TPU v7x, 512 devices: a whole 4x4x16 slice. The times are simulated.
512 devices in a mesh: row: 32 (over y, x, core), col: 16 (over z).
Axes of the slice: x: 4, y: 4, z: 16, core: 2. Of those that a mesh axis runs over, the one named last changes fastest.
Arguments:
- ensemble: float32 [65536, 1024], P(('row', 'col')), may hold values from -6 to 6
- obs_rows: int32 [2, 256], replicated, may hold values from 0 to 127
- owner: int32 [2], replicated, may hold values from 0 to 31
- obs_value: float32 [2, 256], replicated, may hold values from -8 to 8
- obs_var: float32 [2, 256], replicated, may hold values from 0.1 to 2
- taper_mask: int32 [2, 512, 2], P(None, ('row', 'col')), may hold values 0 or 1
Outputs:
- analysis: float32 [65536, 1024], P(('row', 'col'))
Inputs may be any that keep to these rules, and one draw needn't show every extreme that they name: `obs_rows`: observation p of batch b lies on the device at col index p // (256 / 16) of group owner[b]; batches may repeat a group and an observation may repeat a row.
All inputs are finite; a program needn't handle non-finite values. No bound on the sum of `taper_mask` on one device may be relied on, other than what follows from the above.
Results may differ from a plain program's by a relative error of at most 0.00018.
Values sent between devices are 32-bit elements; how exact they have to be, the bound alone decides.
No kernel may reach another device: no remote copies, remote signals or barrier semaphores. Data moves between devices by JAX's collectives and lax.ppermute only.
A program may use at most 64 MiB of HBM per device.

v0:
```python
import jax
import jax.numpy as jnp
from jax import lax
from jax.sharding import PartitionSpec as P

BATCHES = 2


def picked(x, axis, root):
    return lax.dynamic_index_in_dim(lax.all_gather(x, axis), root, 0, keepdims=False)


def from_everyone(x, axis):
    copies = jnp.broadcast_to(x, (lax.axis_size(axis), *x.shape))
    return lax.all_to_all(copies, axis, split_axis=0, concat_axis=0, tiled=True)


def in_order(pieces, dim):
    pieces = jnp.moveaxis(pieces, 0, dim)
    shape = pieces.shape
    return pieces.reshape(*shape[:dim], shape[dim] * shape[dim + 1], *shape[dim + 2 :])


def gathered_copies(x, axis, dim):
    pieces = from_everyone(x, axis)
    return in_order(pieces, dim)


def in_one_piece(arrays, axis, dim, along):
    columns = [a.reshape(*a.shape[:along], -1) for a in arrays]
    both = jnp.concatenate(columns, axis=along)
    filled, at, outs = (gathered_copies(both, axis, dim), 0, [])
    for a, column in zip(arrays, columns):
        slab = filled[..., at : at + column.shape[along]]
        outs.append(slab.reshape(*slab.shape[:along], *a.shape[along:]))
        at += column.shape[along]
    return tuple(outs)


def invert_cov(obs_anom, variances, members):
    count = obs_anom.shape[0]
    cov = jnp.dot(obs_anom, obs_anom.T, precision=lax.Precision.HIGHEST) / (members - 1.0)
    cov = cov + jnp.diag(variances)
    factor = jnp.linalg.cholesky(cov)
    ident = jnp.eye(count, dtype=cov.dtype)
    lower_inv = lax.linalg.triangular_solve(factor, ident, left_side=True, lower=True)
    return lax.linalg.triangular_solve(
        factor, lower_inv, left_side=True, lower=True, transpose_a=True
    )


def on_device(ensemble, obs_rows, owner, obs_value, obs_var, taper_mask):
    rows = ensemble.shape[0]
    members = ensemble.shape[1]
    count = obs_rows.shape[1]
    ncols = lax.axis_size("col")
    nrows = lax.axis_size("row")
    per_dev = count // ncols
    block = rows // taper_mask.shape[1]
    local_len = rows * nrows * ncols // 4
    my_row = lax.axis_index("row")
    my_col = lax.axis_index("col")
    first = (my_row * ncols + my_col) * rows
    positions = first + jnp.arange(rows, dtype=jnp.int32)
    row_ids = jnp.arange(rows, dtype=jnp.int32)
    column_of = jnp.arange(count, dtype=jnp.int32) // per_dev
    state = ensemble
    for batch in range(BATCHES):
        mean = jnp.mean(state, axis=1)
        anom = state - mean[:, None]
        group = owner[batch]
        mine = lax.dynamic_slice_in_dim(obs_rows[batch], my_col * per_dev, per_dev)
        picker = (mine[:, None] == row_ids[None, :]).astype(jnp.float32)
        sel_anom = jnp.dot(picker, anom, precision=lax.Precision.HIGHEST)
        sel_mean = jnp.dot(picker, mean, precision=lax.Precision.HIGHEST)
        share_anom, share_mean = (picked(sel_anom, "row", group), picked(sel_mean, "row", group))
        obs_anom, obs_mean = in_one_piece((share_anom, share_mean), "col", 0, 1)
        cov_inv = invert_cov(obs_anom, obs_var[batch], members)
        glob = (group * ncols + column_of) * rows + obs_rows[batch]
        innov = obs_value[batch] - obs_mean
        blocks = jnp.repeat(jnp.repeat(taper_mask[batch], block, axis=0), block, axis=1)
        dist = jnp.abs(positions[:, None] - glob[None, :]).astype(jnp.float32)
        taper = blocks.astype(jnp.float32) * jnp.exp(-dist / jnp.float32(local_len))
        cross = jnp.dot(anom, obs_anom.T, precision=lax.Precision.HIGHEST) / (members - 1.0)
        gain = jnp.dot(taper * cross, cov_inv, precision=lax.Precision.HIGHEST)
        shift = jnp.dot(gain, innov[:, None], precision=lax.Precision.HIGHEST)
        change = jnp.dot(gain, obs_anom, precision=lax.Precision.HIGHEST)
        state = mean[:, None] + shift + anom - 0.5 * change
    return state


def solution(mesh):
    in_specs = (P(("row", "col"), None), P(), P(), P(), P(), P(None, ("row", "col"), None))
    out_specs = P(("row", "col"), None)
    return jax.shard_map(
        on_device, mesh=mesh, in_specs=in_specs, out_specs=out_specs, check_vma=False
    )
```

profile of v0, /device:TPU:96, one launch (start us, length us, event | category | flops | bytes accessed | tf_op | source)
XLA Modules:
  0.0 543.0 jit_solution(17331332569079020840)
XLA Ops:
  6.5 1.3 fusion.72
  9.1 1.2 reduce_sum.18
  11.1 2.0 fusion.18
  13.8 1.2 dynamic-slice.12
  17.3 128.5 %all-reduce.3 = f32[32,16]{1,0:T(8,128)S(1)} all-reduce(f32[32,16]{1,0:T(8,128)S(1)} %reshape.189), channel_id=3, replica_groups=mesh['row'=32,'col'=16] {'row'}, use_global_device_ids=true, to_apply=%add.1 | all-reduce | flops 512 | bytes 4096
  146.8 1.1 broadcast_in_dim.64
  147.9 14.3 %all-to-all-start = ((f32[16,16,1025]{2,1,0:T(8,128)}), f32[16,16,1025]{2,1,0:T(8,128)S(1)}, u32[]{:S(2)}, u32[]{:S(2)}) async-start(f32[16,16,1025]{2,1,0:T(8,128)} %broadcast_in_dim.64), calls=%async_computation | async-start | bytes 2359296 | tf_op jit(solution)/shard_map/all_to_all | solution.py:15
  162.7 49.9 %all-to-all-done = f32[16,16,1025]{2,1,0:T(8,128)S(1)} async-done(((f32[16,16,1025]{2,1,0:T(8,128)}), f32[16,16,1025]{2,1,0:T(8,128)S(1)}, u32[]{:S(2)}, u32[]{:S(2)}) %all-to-all-start) | async-done | bytes 1049632 | tf_op jit(solution)/shard_map/all_to_all | solution.py:15
  212.5 1.0 fusion.3
  213.8 11.7 %cholesky.130 = f32[128,128]{1,0:T(8,128)S(1)} custom-call(f32[128,128]{1,0:T(8,128)S(1)} %cholesky.194), custom_call_target="Cholesky" | custom-call | tf_op jit(solution)/shard_map/jit(cholesky)/cholesky | solution.py:44
  225.5 9.8 %custom-call.17 = f32[1,128,128]{1,2,0:T(8,128)S(1)} custom-call(f32[1,128,128]{2,1,0:T(8,128)S(1)} %get-tuple-element.67), custom_call_target="InvertDiagBlocksLowerTriangular" | custom-call | tf_op jit(solution)/shard_map/jit(cholesky)/cholesky | solution.py:44
  235.8 11.7 %cholesky.147 = f32[128,128]{1,0:T(8,128)S(1)} custom-call(f32[128,128]{1,0:T(8,128)S(1)} %convolution_subtract_fusion.5), custom_call_target="Cholesky" | custom-call | tf_op jit(solution)/shard_map/jit(cholesky)/cholesky | solution.py:44
  249.7 4.2 while.8
  250.6 1.3 bitcast_dynamic-update-slice_fusion.4
  252.6 1.3 bitcast_dynamic-update-slice_fusion.4
  253.9 19.7 %custom-call.19 = f32[2,128,128]{1,2,0:T(8,128)S(1)} custom-call(f32[2,128,128]{2,1,0:T(8,128)S(1)} %get-tuple-element.37), custom_call_target="InvertDiagBlocksLowerTriangular" | custom-call | tf_op jit(solution)/shard_map/triangular_solve/custom-call.4 | solution.py:47
  275.6 1.2 fusion.5
  278.2 1.0 fusion.15
  281.5 124.5 %all-reduce.4 = f32[32,16]{1,0:T(8,128)S(1)} all-reduce(f32[32,16]{1,0:T(8,128)S(1)} %reshape.191), channel_id=5, replica_groups=mesh['row'=32,'col'=16] {'row'}, use_global_device_ids=true, to_apply=%add.2 | all-reduce | flops 512 | bytes 4096
  407.0 1.1 broadcast_in_dim.70
  408.0 10.3 %all-to-all-start.1 = ((f32[16,16,1025]{2,1,0:T(8,128)}), f32[16,16,1025]{2,1,0:T(8,128)S(1)}, u32[]{:S(2)}, u32[]{:S(2)}) async-start(f32[16,16,1025]{2,1,0:T(8,128)} %broadcast_in_dim.70), calls=%async_computation.1 | async-start | bytes 2359296 | tf_op jit(solution)/shard_map/all_to_all | solution.py:15
  418.6 50.0 %all-to-all-done.1 = f32[16,16,1025]{2,1,0:T(8,128)S(1)} async-done(((f32[16,16,1025]{2,1,0:T(8,128)}), f32[16,16,1025]{2,1,0:T(8,128)S(1)}, u32[]{:S(2)}, u32[]{:S(2)}) %all-to-all-start.1) | async-done | bytes 1049632 | tf_op jit(solution)/shard_map/all_to_all | solution.py:15
  468.6 1.0 fusion.2
  469.8 11.7 %cholesky.164 = f32[128,128]{1,0:T(8,128)S(1)} custom-call(f32[128,128]{1,0:T(8,128)S(1)} %cholesky.197), custom_call_target="Cholesky" | custom-call | tf_op jit(solution)/shard_map/jit(cholesky)/cholesky | solution.py:44
  481.6 9.8 %custom-call.20 = f32[1,128,128]{1,2,0:T(8,128)S(1)} custom-call(f32[1,128,128]{2,1,0:T(8,128)S(1)} %get-tuple-element.63), custom_call_target="InvertDiagBlocksLowerTriangular" | custom-call | tf_op jit(solution)/shard_map/jit(cholesky)/cholesky | solution.py:44
  491.9 11.7 %cholesky.181 = f32[128,128]{1,0:T(8,128)S(1)} custom-call(f32[128,128]{1,0:T(8,128)S(1)} %convolution_subtract_fusion.4), custom_call_target="Cholesky" | custom-call | tf_op jit(solution)/shard_map/jit(cholesky)/cholesky | solution.py:44
  506.4 4.1 while.9
  507.0 1.4 bitcast_dynamic-update-slice_fusion.5
  509.1 1.4 bitcast_dynamic-update-slice_fusion.5
  510.5 19.9 %custom-call.22 = f32[2,128,128]{1,2,0:T(8,128)S(1)} custom-call(f32[2,128,128]{2,1,0:T(8,128)S(1)} %get-tuple-element.39), custom_call_target="InvertDiagBlocksLowerTriangular" | custom-call | tf_op jit(solution)/shard_map/triangular_solve/custom-call.4 | solution.py:47
  532.4 1.2 fusion.4
  534.1 1.6 fusion.1
  (96 shorter events, 16.2 us)
Async XLA Ops:
  6.5 139.4 %all-gather.7.cloned.1.call-start = ((), (), s32[]{:S(2)}) async-start(), calls=%async_computation.2 | async-start | bytes 2162688 | tf_op jit(solution)/shard_map/all_gather | solution.py:10
  147.9 14.4 %copy-start.1 = (f32[2,256]{1,0:T(2,128)S(1)}, f32[2,256]{1,0:T(2,128)}, u32[]{:S(2)}) copy-start(f32[2,256]{1,0:T(2,128)} %param.14) | copy-start | bytes 6148
  147.9 14.7 %copy-start.3 = (s32[2,1,2]{2,1,0:T(1,128)S(1)}, s32[2,1,2]{2,1,0:T(1,128)}, u32[]{:S(2)}) copy-start(s32[2,1,2]{2,1,0:T(1,128)} %param.16) | copy-start | bytes 52
  147.9 14.8 %copy-start.2 = (f32[2,256]{1,0:T(2,128)S(1)}, f32[2,256]{1,0:T(2,128)}, u32[]{:S(2)}) copy-start(f32[2,256]{1,0:T(2,128)} %param.15) | copy-start | bytes 6148
  147.9 64.7 %all-to-all-start = ((f32[16,16,1025]{2,1,0:T(8,128)}), f32[16,16,1025]{2,1,0:T(8,128)S(1)}, u32[]{:S(2)}, u32[]{:S(2)}) async-start(f32[16,16,1025]{2,1,0:T(8,128)} %broadcast_in_dim.64), calls=%async_computation | async-start | bytes 2359296 | tf_op jit(solution)/shard_map/all_to_all | solution.py:15
  162.2 243.9 %all-gather.9.cloned.1.call-start = ((), (), s32[]{:S(2)}) async-start(), calls=%async_computation.3 | async-start | bytes 2162688 | tf_op jit(solution)/shard_map/all_gather | solution.py:10
  273.6 2.0 copy-start
  408.0 60.5 %all-to-all-start.1 = ((f32[16,16,1025]{2,1,0:T(8,128)}), f32[16,16,1025]{2,1,0:T(8,128)S(1)}, u32[]{:S(2)}, u32[]{:S(2)}) async-start(f32[16,16,1025]{2,1,0:T(8,128)} %broadcast_in_dim.70), calls=%async_computation.1 | async-start | bytes 2359296 | tf_op jit(solution)/shard_map/all_to_all | solution.py:15
Sparse Core Ops, SparseCore 0:
  13.3 62.2 all-gather.6
  279.4 53.2 all-gather.8
where the time goes:
time: 553 us; the launch traced here: 543 us
  blocking collectives  253 us (46%)
  other arithmetic  111 us (20%)
  waiting for transfers between devices  99.9 us (18%)
  starting transfers between devices  24.7 us (4%)
  between operations  22.3 us (4%)
  local copies, waits for them, and re-layouts  16.2 us (3%)
  matrix products  15.9 us (3%)
    unnamed x2, blocking collectives  253 us
    all_to_all x2, waiting for transfers between devices, from_everyone(): return lax.all_to_all(copies, axis, split_axis=0, concat_axis=0, tiled=True)  99.9 us
    another operation x13, other arithmetic, invert_cov(): factor = jnp.linalg.cholesky(cov)  68.7 us
    another operation x5, other arithmetic, invert_cov(): lax.linalg.triangular_solve(factor, lower_inv, left_side=True, lower=True...  39.7 us
    all_to_all x2, starting transfers between devices, from_everyone(): return lax.all_to_all(copies, axis, split_axis=0, concat_axis=0, tiled=True)  24.7 us
  transfers between devices with their start and end apart: 4, of which 2 were waited for; matrix products, arithmetic and copies ran while one was open for 1% of the time, Pallas kernels for 0%

commit v1 on v0

v1 whole, which is shorter than its diff:
```python
import functools

import jax
import jax.numpy as jnp
from jax import lax
from jax.experimental import pallas as pl
from jax.experimental.pallas import tpu as pltpu
from jax.sharding import PartitionSpec as P

HIGHEST = lax.Precision.HIGHEST
VMEM = pltpu.VMEM
SMEM = pltpu.SMEM
PIVOTS = 32


def spread(x, row):
    return jnp.broadcast_to(x[row : row + 1, :], (8, 128))


def sweep_panel(panel, base, lanes, subs):
    high = base >= 128
    q0 = base - jnp.where(high, 128, 0)
    low_half = [panel[8 * g : 8 * g + 8, :128] for g in range(4)]
    high_half = [panel[8 * g : 8 * g + 8, 128:] for g in range(4)]
    act = [jnp.where(high, h, l) for l, h in zip(low_half, high_half)]
    oth = [jnp.where(high, l, h) for l, h in zip(low_half, high_half)]
    for sb in range(4):
        cols = []
        for l in range(8):
            index = jnp.full((8, 128), q0 + (8 * sb + l), jnp.int32)
            cols.append([jnp.take_along_axis(act[g], index, axis=1) for g in range(4)])
        for l in range(8):
            u = cols[l]
            at_row = subs == l
            at_lane = lanes == q0 + (8 * sb + l)
            inv = 1.0 / spread(u[sb], l)
            for m in range(l + 1, 8):
                t = spread(cols[m][sb], l) * inv
                new = [cols[m][g] - u[g] * t for g in range(4)]
                new[sb] = jnp.where(at_row, t, new[sb])
                cols[m] = new
            row_act = jnp.where(at_lane, -inv, spread(act[sb], l) * inv)
            row_oth = spread(oth[sb], l) * inv
            act = [jnp.where(at_lane, 0.0, act[g]) - u[g] * row_act for g in range(4)]
            oth = [oth[g] - u[g] * row_oth for g in range(4)]
            act[sb] = jnp.where(at_row, row_act, act[sb])
            oth[sb] = jnp.where(at_row, row_oth, oth[sb])
    act, oth = jnp.concatenate(act, 0), jnp.concatenate(oth, 0)
    return jnp.concatenate(
        [jnp.where(high, oth, act), jnp.where(high, act, oth)], axis=1
    )


def invert_in_place(a_ref):
    n = a_ref.shape[0]
    lanes = lax.broadcasted_iota(jnp.int32, (8, 128), 1)
    subs = lax.broadcasted_iota(jnp.int32, (8, 128), 0)
    columns = lax.broadcasted_iota(jnp.int32, (n, n), 1)

    def outer(k, carry):
        base = pl.multiple_of(k * PIVOTS, PIVOTS)
        panel = a_ref[pl.ds(base, PIVOTS), :]
        swept = sweep_panel(panel, base, lanes, subs)
        prod = lax.dot_general(
            panel.T, swept, (((1,), (0,)), ((), ())), precision=HIGHEST,
            preferred_element_type=jnp.float32,
        )
        inside = (columns >= base) & (columns < base + PIVOTS)
        a_ref[...] = jnp.where(inside, 0.0, a_ref[...]) - prod
        a_ref[pl.ds(base, PIVOTS), :] = swept
        return carry

    lax.fori_loop(0, n // PIVOTS, outer, 0)


def dot_nt(a, b):
    return lax.dot_general(
        a, b, (((1,), (1,)), ((), ())), precision=HIGHEST,
        preferred_element_type=jnp.float32,
    )


def dot_nn(a, b):
    return jnp.dot(a, b, precision=HIGHEST, preferred_element_type=jnp.float32)


def pick_kernel(rows_ref, col_ref, mask_ref, x_ref, out_ref, held):
    rows_dev, members = x_ref.shape
    count = rows_ref.shape[1]
    per_dev = held.shape[0] // 2
    start = col_ref[0] * per_dev
    for b in range(2):
        for i in range(per_dev):
            r = rows_ref[b, start + i]
            held[b * per_dev + i : b * per_dev + i + 1, :] = x_ref[pl.ds(r, 1), :]
    chunks = members // 128
    subs = lax.broadcasted_iota(jnp.int32, (8, 128), 0)
    kept = jnp.where(subs == 0, mask_ref[0, 0, 0], mask_ref[0, 0, 1]).astype(jnp.float32)
    for piece in range(out_ref.shape[0]):
        g, j = piece // chunks, piece % chunks
        out_ref[piece, :8, :] = held[8 * g : 8 * g + 8, 128 * j : 128 * j + 128]
        out_ref[piece, 8:, :] = kept


def assimilate_kernel(
    place_ref, owner_ref, mask_ref, x_ref, own_ref, other_ref, kept_ref,
    rows_ref, rows_col_ref, value_col_ref, var_ref,
    out_ref, q_ref, t_ref, c_ref, g_ref, mean_ref,
    *, ncols, local_len,
):
    rows_dev, members = x_ref.shape
    n = rows_ref.shape[1]
    per_dev = n // ncols
    chunks = members // 128
    core, first = place_ref[0], place_ref[1]
    scale = 1.0 / (members - 1.0)
    obs1, obs0 = rows_dev, rows_dev + n

    def unpack(c, carry):
        for b, top in ((0, obs0), (1, obs1)):
            for gg in range(per_dev // 8):
                for jj in range(chunks // 2):
                    slot = (b * (per_dev // 8) + gg) * (chunks // 2) + jj
                    at = pl.ds(pl.multiple_of(top + c * per_dev + gg * 8, 8), 8)
                    mine = pl.multiple_of((2 * jj + core) * 128, 128)
                    theirs = pl.multiple_of((2 * jj + 1 - core) * 128, 128)
                    q_ref[at, pl.ds(mine, 128)] = own_ref[slot, c]
                    q_ref[at, pl.ds(theirs, 128)] = other_ref[slot, c]
        return carry

    lax.fori_loop(0, ncols, unpack, 0)
    q_ref[:rows_dev, :] = x_ref[...]

    def centre(i, carry):
        at = pl.ds(pl.multiple_of(i * 64, 64), 64)
        x = q_ref[at, :]
        mean = jnp.sum(x, axis=1, keepdims=True) * (1.0 / members)
        mean_ref[at, :] = jnp.broadcast_to(mean, (64, 128))
        q_ref[at, :] = x - mean
        return carry

    lax.fori_loop(0, q_ref.shape[0] // 64, centre, 0)

    lane = lax.broadcasted_iota(jnp.int32, (1, n), 1)
    glob = [(owner_ref[b] * ncols + lane // per_dev) * rows_dev + rows_ref[b : b + 1, :] for b in range(2)]
    diag = lax.broadcasted_iota(jnp.int32, (n, n), 0) == lax.broadcasted_iota(jnp.int32, (n, n), 1)
    here = first + lax.broadcasted_iota(jnp.int32, (rows_dev, 1), 0)
    sub = lax.broadcasted_iota(jnp.int32, (n, 1), 0)
    there = (owner_ref[1] * ncols + sub // per_dev) * rows_dev + rows_col_ref[:, 1:2]

    def decay(positions, b):
        dist = jnp.abs(positions - glob[b]).astype(jnp.float32)
        return jnp.exp(-dist / jnp.float32(local_len))

    def local_mask(b):
        return jnp.where(lane < 128, mask_ref[b, 0, 0], mask_ref[b, 0, 1]).astype(jnp.float32)

    def cross0(i, carry):
        at = pl.ds(pl.multiple_of(i * 128, 128), 128)
        t_ref[at, :] = dot_nt(q_ref[at, :], q_ref[obs0:, :]) * scale
        return carry

    lax.fori_loop(0, q_ref.shape[0] // 128, cross0, 0)
    c_ref[...] = t_ref[obs0:, :] + jnp.where(diag, var_ref[0:1, :], 0.0)
    invert_in_place(c_ref)

    t_ref[:rows_dev, :] = t_ref[:rows_dev, :] * (decay(here, 0) * local_mask(0))
    for c in range(ncols):
        at = slice(obs1 + c * per_dev, obs1 + (c + 1) * per_dev)
        kept = jnp.concatenate(
            [jnp.broadcast_to(kept_ref[c, i : i + 1, :], (per_dev, 128)) for i in range(2)], axis=1
        )
        t_ref[at, :] = t_ref[at, :] * (decay(there[c * per_dev : (c + 1) * per_dev], 0) * kept)
    innov0 = value_col_ref[:, 0:1] - mean_ref[obs0:, :]

    def update(i, carry):
        at = pl.ds(pl.multiple_of(i * 128, 128), 128)
        gain = -dot_nn(t_ref[at, :], c_ref[...])
        mean_ref[at, :] = mean_ref[at, :] + dot_nn(gain, innov0)
        q_ref[at, :] = q_ref[at, :] - 0.5 * dot_nn(gain, q_ref[obs0:, :])
        return carry

    lax.fori_loop(0, obs0 // 128, update, 0)

    def cross1(i, carry):
        at = pl.ds(pl.multiple_of(i * 128, 128), 128)
        t_ref[at, :] = dot_nt(q_ref[at, :], q_ref[obs1:obs0, :]) * scale
        return carry

    lax.fori_loop(0, obs0 // 128, cross1, 0)
    c_ref[...] = t_ref[obs1:obs0, :] + jnp.where(diag, var_ref[1:2, :], 0.0)
    invert_in_place(c_ref)
    innov1 = value_col_ref[:, 1:2] - mean_ref[obs1:obs0, :]
    tapered = t_ref[:rows_dev, :] * (decay(here, 1) * local_mask(1))
    gain = -dot_nn(tapered, c_ref[...])
    mean = mean_ref[:rows_dev, :] + dot_nn(gain, innov1)
    change = dot_nn(gain, q_ref[obs1:obs0, :])
    out_ref[...] = mean[:, 0:1] + q_ref[:rows_dev, :] - 0.5 * change


def to_all(x, axis, copies, groups=None):
    wide = jnp.broadcast_to(x[None], (copies, *x.shape))
    return lax.all_to_all(wide, axis, split_axis=0, concat_axis=0, axis_index_groups=groups, tiled=True)


def pick_rows(ensemble, obs_rows, taper_mask, my_col, per_dev):
    members = ensemble.shape[1]
    pieces = 2 * per_dev // 8 * (members // 128)
    return pl.pallas_call(
        pick_kernel,
        out_shape=jax.ShapeDtypeStruct((pieces, 16, 128), jnp.float32),
        in_specs=[pl.BlockSpec(memory_space=SMEM)] * 3 + [pl.BlockSpec(memory_space=VMEM)],
        out_specs=pl.BlockSpec(memory_space=VMEM),
        scratch_shapes=[VMEM((2 * per_dev, members), jnp.float32)],
        name="pick_rows",
    )(obs_rows, my_col[None], taper_mask, ensemble)


def assimilate(place, owner, taper_mask, ensemble, own, other, kept, obs_rows, obs_value, obs_var, ncols, local_len):
    rows_dev, members = ensemble.shape
    n = obs_rows.shape[1]
    total = rows_dev + 2 * n
    return pl.pallas_call(
        functools.partial(assimilate_kernel, ncols=ncols, local_len=local_len),
        out_shape=jax.ShapeDtypeStruct(ensemble.shape, jnp.float32),
        in_specs=[pl.BlockSpec(memory_space=SMEM)] * 3 + [pl.BlockSpec(memory_space=VMEM)] * 8,
        out_specs=pl.BlockSpec(memory_space=VMEM),
        scratch_shapes=[
            VMEM((total, members), jnp.float32),
            VMEM((total, n), jnp.float32),
            VMEM((n, n), jnp.float32),
            VMEM((8, 128), jnp.float32),
            VMEM((total, 128), jnp.float32),
        ],
        compiler_params=pltpu.CompilerParams(vmem_limit_bytes=40 * 1024 * 1024),
        name="assimilate",
    )(place, owner, taper_mask, ensemble, own, other, kept, obs_rows, obs_rows.T, obs_value.T, obs_var)


def gather_observed(ensemble, obs_rows, owner, taper_mask, my_row, my_col, nrows, ncols):
    per_dev = obs_rows.shape[1] // ncols
    picked = pick_rows(ensemble, obs_rows, taper_mask, my_col, per_dev)
    spread_out = lax.all_to_all(picked, "row", split_axis=0, concat_axis=0, tiled=True)
    batch = my_row // (nrows // 2)
    data = lax.dynamic_index_in_dim(spread_out, owner[batch], 0, keepdims=False)[:8]
    kept = lax.dynamic_index_in_dim(spread_out, owner[1], 0, keepdims=False)[8:]
    line = to_all(jnp.concatenate([data, kept], 0), "col", ncols)
    line = line.reshape(ncols, 16, 128)
    same_core = [[r for r in range(nrows) if r % 2 == c] for c in range(2)]
    own = to_all(line[:, :8], "row", nrows // 2, same_core).reshape(nrows // 2, ncols, 8, 128)
    other = lax.ppermute(own, "row", [(r, r ^ 1) for r in range(nrows)])
    return own, other, line[:, 8:]


def on_device(ensemble, obs_rows, owner, obs_value, obs_var, taper_mask):
    rows = ensemble.shape[0]
    ncols, nrows = lax.axis_size("col"), lax.axis_size("row")
    my_row, my_col = lax.axis_index("row"), lax.axis_index("col")
    own, other, kept = gather_observed(ensemble, obs_rows, owner, taper_mask, my_row, my_col, nrows, ncols)
    local_len = rows * nrows * ncols // 4
    place = jnp.stack([my_row % 2, (my_row * ncols + my_col) * rows]).astype(jnp.int32)
    return assimilate(place, owner, taper_mask, ensemble, own, other, kept, obs_rows, obs_value, obs_var, ncols, local_len)


def solution(mesh):
    in_specs = (P(("row", "col"), None), P(), P(), P(), P(), P(None, ("row", "col"), None))
    out_specs = P(("row", "col"), None)
    return jax.shard_map(
        on_device, mesh=mesh, in_specs=in_specs, out_specs=out_specs, check_vma=False
    )
```

time: 553 us -> 110 us (0.20)
  the two profiles are of different devices: /device:TPU:96 before, /device:TPU:1 now
where the time goes in v1:
time: 110 us
  blocking collectives  42.3 us (38%)
  Pallas kernels  38.7 us (35%)
  starting transfers between devices  16.4 us (15%)
  waiting for transfers between devices  4.64 us (4%)
  between operations  3.72 us (3%)
  local copies, waits for them, and re-layouts  3.67 us (3%)
    all_to_all x2, blocking collectives, to_all(): lax.all_to_all(wide, axis, split_axis=0, concat_axis=0, axis_index_groups...  42.3 us
    pallas_call x1, Pallas kernels, assimilate(): pl.pallas_call(functools.partial(assimilate_kernel, ncols=ncols, local_le...  36.9 us
    all_to_all x1, starting transfers between devices, gather_observed(): lax.all_to_all(picked, 'row', split_axis=0, concat_axis=0, tiled=True)  10.4 us
    ppermute x1, starting transfers between devices, gather_observed(): other = lax.ppermute(own, 'row', [(r, r ^ 1) for r in range(nrows)])  6.05 us
    all_to_all x1, waiting for transfers between devices, gather_observed(): lax.all_to_all(picked, 'row', split_axis=0, concat_axis=0, tiled=True)  4.12 us
    unnamed x14, local copies, waits for them, and re-layouts  2.95 us
  transfers between devices with their start and end apart: 2, of which 2 were waited for; matrix products, arithmetic and copies ran while one was open for 1% of the time, Pallas kernels for 0%

profile of v1, /device:TPU:1, one launch (start us, length us, event | category | flops | bytes accessed | tf_op | source)
XLA Modules:
  0.0 109.5 jit_solution(16616531989005427811)
XLA Ops:
  0.0 1.9 %pick_rows.1 = f32[32,16,128]{2,1,0:T(8,128)} custom-call(s32[2,256]{1,0:T(2,128)} %rows_ref.3, s32[1]{0:T(128)} %bitcast.2.col_ref, s32[2,1,2]{2,1,0:T(1,128)} %mask_ref.3, f32[128,1024]{1,0:T(8,128)} %x_ref.3), custom_call_target="tpu_custom_call" | custom-call | tf_op jit(solution)/shard_map/pick_rows/pallas_call | solution.py:209
  1.9 10.4 %all-to-all-start = ((f32[32,16,128]{2,1,0:T(8,128)}), f32[32,16,128]{2,1,0:T(8,128)S(1)}, u32[]{:S(2)}, u32[]{:S(2)}) async-start(f32[32,16,128]{2,1,0:T(8,128)} %pick_rows.1), calls=%async_computation | async-start | bytes 524288 | tf_op jit(solution)/shard_map/all_to_all | solution.py:243
  12.3 0.0 copy-start.2
  12.3 0.6 copy-done.2
  12.9 0.6 fusion.1
  17.1 4.1 %all-to-all-done = f32[32,16,128]{2,1,0:T(8,128)S(1)} async-done(((f32[32,16,128]{2,1,0:T(8,128)}), f32[32,16,128]{2,1,0:T(8,128)S(1)}, u32[]{:S(2)}, u32[]{:S(2)}) %all-to-all-start) | async-done | bytes 262176 | tf_op jit(solution)/shard_map/all_to_all | solution.py:243
  21.3 24.9 %all_to_all.15 = f32[16,16,128]{2,1,0:T(8,128)S(1)} all-to-all(f32[16,16,128]{2,1,0:T(8,128)S(1)} %broadcast_in_dim.7), channel_id=1, replica_groups=mesh['row'=32,'col'=16] {'col'}, dimensions={0} | all-to-all | bytes 262144 | tf_op jit(solution)/shard_map/all_to_all | solution.py:203
  46.2 0.1 broadcast_in_dim.8
  46.3 0.0 copy-start
  46.3 17.3 %all_to_all.16.own_ref = f32[16,16,8,128]{3,2,1,0:T(8,128)S(1)} all-to-all(f32[16,16,8,128]{3,2,1,0:T(8,128)S(1)} %broadcast_in_dim.8), channel_id=1, replica_groups={{0,32,64,96,128,160,192,224,256,288,320,352,384,416,448,480},{16,48,80,..., dimensions={0} | all-to-all | bytes 2097152 | tf_op jit(solution)/shard_map/all_to_all | solution.py:203
  63.7 6.1 %collective-permute-start = (f32[16,16,8,128]{3,2,1,0:T(8,128)S(1)}, f32[16,16,8,128]{3,2,1,0:T(8,128)S(1)}, u32[]{:S(2)}, u32[]{:S(2)}) collective-permute-start(f32[16,16,8,128]{3,2,1,0:T(8,128)S(1)} %all_to_all.16.own_ref), channel_id=1, source_target_pairs={{0,16},{16,0},{32,48},{48,32},{64,80},{80,64},{96,112},{112,96},{1... | collective-permute-start | bytes 3145736 | tf_op jit(solution)/shard_map/ppermute | solution.py:251
  69.7 0.0 copy-start.1
  69.7 0.7 copy-done.1
  70.4 0.1 copy.7
  70.6 0.0 copy-start.5
  70.6 0.7 copy-done.5
  71.2 0.1 copy.8
  71.4 0.1 pad_add_fusion.place_ref
  71.5 0.5 collective-permute-done.other_ref
  72.0 0.0 copy-start.4
  72.0 0.0 copy-start.3
  72.0 0.0 copy-done
  72.0 0.7 copy-done.4
  72.7 0.0 copy-done.3
  72.7 36.9 %assimilate.1 = f32[128,1024]{1,0:T(8,128)} custom-call(s32[2]{0:T(128)S(1)} %pad_add_fusion.place_ref, s32[2]{0:T(128)S(1)} %copy-done.2, s32[2,1,2]{2,1,0:T(1,128)S(1)} %copy-done.3, f32[128,1024]{1,0:T(8,128)S(1)} %copy-done, f32[16,16,8,128]{3,2,1,0:T(8,128)S(1)} %all_to_all.16.own_ref, f32[16,16,8,128]{3,2,1,0:T(8,128)S(1)} %collective-permute-done.other_ref, ...), custom_call_target="tpu_custom_call" | custom-call | tf_op jit(solution)/shard_map/assimilate/pallas_call | solution.py:223
  (4 shorter events, 0.0 us)
Async XLA Ops:
  1.9 19.4 %all-to-all-start = ((f32[32,16,128]{2,1,0:T(8,128)}), f32[32,16,128]{2,1,0:T(8,128)S(1)}, u32[]{:S(2)}, u32[]{:S(2)}) async-start(f32[32,16,128]{2,1,0:T(8,128)} %pick_rows.1), calls=%async_computation | async-start | bytes 524288 | tf_op jit(solution)/shard_map/all_to_all | solution.py:243
  12.3 0.7 copy-start.2
  46.3 25.7 %copy-start = (f32[128,1024]{1,0:T(8,128)S(1)}, f32[128,1024]{1,0:T(8,128)}, u32[]{:S(2)}) copy-start(f32[128,1024]{1,0:T(8,128)} %x_ref.3) | copy-start | bytes 1572868
  63.7 8.3 %collective-permute-start = (f32[16,16,8,128]{3,2,1,0:T(8,128)S(1)}, f32[16,16,8,128]{3,2,1,0:T(8,128)S(1)}, u32[]{:S(2)}, u32[]{:S(2)}) collective-permute-start(f32[16,16,8,128]{3,2,1,0:T(8,128)S(1)} %all_to_all.16.own_ref), channel_id=1, source_target_pairs={{0,16},{16,0},{32,48},{48,32},{64,80},{80,64},{96,112},{112,96},{1... | collective-permute-start | bytes 3145736 | tf_op jit(solution)/shard_map/ppermute | solution.py:251
  69.7 0.7 copy-start.1
  70.6 0.7 copy-start.5
  72.0 0.7 copy-start.4
  72.0 0.7 copy-start.3

commit v2 on v1

--- a/solution.py
+++ b/solution.py
@@ -7,10 +7,37 @@
 from jax.experimental.pallas import tpu as pltpu
 from jax.sharding import PartitionSpec as P
 
-HIGHEST = lax.Precision.HIGHEST
 VMEM = pltpu.VMEM
 SMEM = pltpu.SMEM
 PIVOTS = 32
+TERMS = ((0, 0), (0, 1), (1, 0), (1, 1), (0, 2), (2, 0))
+
+
+def split(x, parts):
+    out = []
+    for i in range(parts):
+        out.append(x.astype(jnp.bfloat16))
+        if i < parts - 1:
+            x = x - out[-1].astype(jnp.float32)
+    return out
+
+
+def dot_parts(a, b, contract):
+    pairs = TERMS[: 3 if len(a) == 2 else 6]
+    left = jnp.concatenate([a[i] for i, _ in pairs], axis=1)
+    right = jnp.concatenate([b[j] for _, j in pairs], axis=contract)
+    return lax.dot_general(
+        left, right, (((1,), (contract,)), ((), ())), preferred_element_type=jnp.float32
+    )
+
+
+def by_terms(x, side):
+    parts = split(x, 3)
+    return jnp.concatenate([parts[term[side]] for term in TERMS], axis=0)
+
+
+def one_pass(a, b):
+    return jnp.dot(a, b, preferred_element_type=jnp.float32)
 
 
 def spread(x, row):
@@ -24,64 +51,100 @@
     high_half = [panel[8 * g : 8 * g + 8, 128:] for g in range(4)]
     act = [jnp.where(high, h, l) for l, h in zip(low_half, high_half)]
     oth = [jnp.where(high, l, h) for l, h in zip(low_half, high_half)]
+
+    def column(g, c):
+        return jnp.take_along_axis(act[g], jnp.full((8, 128), q0 + c, jnp.int32), axis=1)
+
+    diag = [column(0, l) for l in range(8)]
     for sb in range(4):
-        cols = []
+        cols = [[None] * 4 for _ in range(8)]
+        later = [g for g in range(sb + 1, 4)] + [g for g in range(sb)]
+        for g in later[:1]:
+            for l in range(8):
+                cols[l][g] = column(g, 8 * sb + l)
+        following = [column(sb + 1, 8 * sb + 8 + l) for l in range(8)] if sb < 3 else None
+        for g in later[1:]:
+            for l in range(8):
+                cols[l][g] = column(g, 8 * sb + l)
+        invs, factors = [], [[None] * 8 for _ in range(8)]
         for l in range(8):
-            index = jnp.full((8, 128), q0 + (8 * sb + l), jnp.int32)
-            cols.append([jnp.take_along_axis(act[g], index, axis=1) for g in range(4)])
+            at_row = subs == l
+            inv = 1.0 / spread(diag[l], l)
+            invs.append(inv)
+            for m in range(l + 1, 8):
+                t = spread(diag[m], l) * inv
+                factors[l][m] = t
+                diag[m] = jnp.where(at_row, t, diag[m] - diag[l] * t)
+        for l in range(8):
+            cols[l][sb] = diag[l]
+        for g in later:
+            for l in range(8):
+                for m in range(l + 1, 8):
+                    cols[m][g] = cols[m][g] - cols[l][g] * factors[l][m]
+        if sb < 3:
+            for l in range(8):
+                scaled = cols[l][sb + 1] * invs[l]
+                following = [f - cols[l][sb + 1] * spread(scaled, m) for m, f in enumerate(following)]
         for l in range(8):
             u = cols[l]
             at_row = subs == l
             at_lane = lanes == q0 + (8 * sb + l)
-            inv = 1.0 / spread(u[sb], l)
-            for m in range(l + 1, 8):
-                t = spread(cols[m][sb], l) * inv
-                new = [cols[m][g] - u[g] * t for g in range(4)]
-                new[sb] = jnp.where(at_row, t, new[sb])
-                cols[m] = new
+            inv = invs[l]
             row_act = jnp.where(at_lane, -inv, spread(act[sb], l) * inv)
             row_oth = spread(oth[sb], l) * inv
             act = [jnp.where(at_lane, 0.0, act[g]) - u[g] * row_act for g in range(4)]
             oth = [oth[g] - u[g] * row_oth for g in range(4)]
             act[sb] = jnp.where(at_row, row_act, act[sb])
             oth[sb] = jnp.where(at_row, row_oth, oth[sb])
+        diag = following
     act, oth = jnp.concatenate(act, 0), jnp.concatenate(oth, 0)
     return jnp.concatenate(
         [jnp.where(high, oth, act), jnp.where(high, act, oth)], axis=1
     )
 
 
-def invert_in_place(a_ref):
+def invert_in_place(a_ref, panel_ref, swept_ref, trans_ref, beside):
     n = a_ref.shape[0]
+    steps = n // PIVOTS
     lanes = lax.broadcasted_iota(jnp.int32, (8, 128), 1)
     subs = lax.broadcasted_iota(jnp.int32, (8, 128), 0)
     columns = lax.broadcasted_iota(jnp.int32, (n, n), 1)
 
-    def outer(k, carry):
-        base = pl.multiple_of(k * PIVOTS, PIVOTS)
-        panel = a_ref[pl.ds(base, PIVOTS), :]
-        swept = sweep_panel(panel, base, lanes, subs)
-        prod = lax.dot_general(
-            panel.T, swept, (((1,), (0,)), ((), ())), precision=HIGHEST,
-            preferred_element_type=jnp.float32,
-        )
-        inside = (columns >= base) & (columns < base + PIVOTS)
-        a_ref[...] = jnp.where(inside, 0.0, a_ref[...]) - prod
-        a_ref[pl.ds(base, PIVOTS), :] = swept
-        return carry
-
-    lax.fori_loop(0, n // PIVOTS, outer, 0)
-
-
-def dot_nt(a, b):
-    return lax.dot_general(
-        a, b, (((1,), (1,)), ((), ())), precision=HIGHEST,
-        preferred_element_type=jnp.float32,
-    )
-
-
-def dot_nn(a, b):
-    return jnp.dot(a, b, precision=HIGHEST, preferred_element_type=jnp.float32)
+    def inside(k, rows):
+        return (columns[:rows] >= k * PIVOTS) & (columns[:rows] < (k + 1) * PIVOTS)
+
+    def rows_of(k):
+        return pl.ds(pl.multiple_of(k * PIVOTS, PIVOTS), PIVOTS)
+
+    def apply(k, slot):
+        a_ref[...] = jnp.where(inside(k, n), 0.0, a_ref[...]) - one_pass(
+            trans_ref[slot], by_terms(swept_ref[slot], 1)
+        )
+
+    panel_ref[...] = a_ref[:PIVOTS, :]
+    swept_ref[1] = jnp.zeros_like(panel_ref)
+    trans_ref[1] = jnp.zeros(trans_ref.shape[1:], jnp.bfloat16)
+
+    def step(k, carry):
+        now, before = k % 2, (k + 1) % 2
+        panel = panel_ref[...]
+        trans_ref[now] = by_terms(panel, 0).T
+        swept = sweep_panel(panel, k * PIVOTS, lanes, subs)
+        apply(k - 1, before)
+        last = jnp.maximum(k - 1, 0)
+        a_ref[rows_of(last), :] = jnp.where(k > 0, swept_ref[before], a_ref[rows_of(last), :])
+        beside(k)
+        following = jnp.minimum(k + 1, steps - 1)
+        panel_ref[...] = jnp.where(inside(k, PIVOTS), 0.0, a_ref[rows_of(following), :]) - one_pass(
+            trans_ref[now, rows_of(following), :], by_terms(swept, 1)
+        )
+        swept_ref[now] = swept
+        return carry
+
+    lax.fori_loop(0, steps, step, 0)
+    final = (steps - 1) % 2
+    apply(steps - 1, final)
+    a_ref[n - PIVOTS :, :] = swept_ref[final]
 
 
 def pick_kernel(rows_ref, col_ref, mask_ref, x_ref, out_ref, held):
@@ -105,7 +168,8 @@
 def assimilate_kernel(
     place_ref, owner_ref, mask_ref, x_ref, own_ref, other_ref, kept_ref,
     rows_ref, rows_col_ref, value_col_ref, var_ref,
-    out_ref, q_ref, t_ref, c_ref, g_ref, mean_ref,
+    out_ref, q_ref, s0_ref, s1_ref, t_ref, c_ref, g_ref, mean_ref, panel_ref, swept_ref, trans_ref,
+    v_ref, innov_ref,
     *, ncols, local_len,
 ):
     rows_dev, members = x_ref.shape
@@ -119,50 +183,68 @@
     def unpack(c, carry):
         for b, top in ((0, obs0), (1, obs1)):
             for gg in range(per_dev // 8):
+                at = pl.ds(pl.multiple_of(top + c * per_dev + gg * 8, 8), 8)
+                total = jnp.zeros((8, 128), jnp.float32)
                 for jj in range(chunks // 2):
                     slot = (b * (per_dev // 8) + gg) * (chunks // 2) + jj
-                    at = pl.ds(pl.multiple_of(top + c * per_dev + gg * 8, 8), 8)
                     mine = pl.multiple_of((2 * jj + core) * 128, 128)
                     theirs = pl.multiple_of((2 * jj + 1 - core) * 128, 128)
                     q_ref[at, pl.ds(mine, 128)] = own_ref[slot, c]
                     q_ref[at, pl.ds(theirs, 128)] = other_ref[slot, c]
+                    total = total + (own_ref[slot, c] + other_ref[slot, c])
+                mean_ref[at, :] = total
         return carry
 
     lax.fori_loop(0, ncols, unpack, 0)
-    q_ref[:rows_dev, :] = x_ref[...]
-
-    def centre(i, carry):
-        at = pl.ds(pl.multiple_of(i * 64, 64), 64)
-        x = q_ref[at, :]
-        mean = jnp.sum(x, axis=1, keepdims=True) * (1.0 / members)
-        mean_ref[at, :] = jnp.broadcast_to(mean, (64, 128))
-        q_ref[at, :] = x - mean
-        return carry
-
-    lax.fori_loop(0, q_ref.shape[0] // 64, centre, 0)
+    total = x_ref[:, :128]
+    for j in range(1, chunks):
+        total = total + x_ref[:, 128 * j : 128 * j + 128]
+    mean_ref[:rows_dev, :] = total
+    mean = jnp.sum(mean_ref[...], axis=1, keepdims=True) * (1.0 / members)
+    mean_ref[...] = jnp.broadcast_to(mean, mean_ref.shape)
+
+    def chunk(j, width):
+        return pl.ds(pl.multiple_of(j * width, width), width)
+
+    wide = 2 * 128
+    diag = lax.broadcasted_iota(jnp.int32, (n, n), 0) == lax.broadcasted_iota(jnp.int32, (n, n), 1)
+    c_ref[...] = jnp.where(diag, var_ref[0:1, :], 0.0)
+
+    def covariance0(j, carry):
+        at = chunk(j, wide)
+        anom = q_ref[obs0:, at] - jnp.concatenate([mean_ref[obs0:, :]] * 2, axis=1)
+        parts = split(anom, 3)
+        for i in range(3):
+            s0_ref[i, :, at] = parts[i]
+        c_ref[...] += dot_parts(parts, parts, 1) * scale
+        return carry
+
+    lax.fori_loop(0, members // wide, covariance0, 0)
+    t_ref[...] = jnp.zeros_like(t_ref)
+
+    def cross0(j):
+        at = chunk(j, 128)
+        for top, rows, src in ((0, rows_dev, x_ref), (obs1, n, q_ref)):
+            anom = src[top : top + rows, at] - mean_ref[top : top + rows, :]
+            q_ref[top : top + rows, at] = anom
+            t_ref[top : top + rows, :] += dot_parts(
+                split(anom, 3), [s0_ref[i, :, at] for i in range(3)], 1
+            )
+
+    invert_in_place(c_ref, panel_ref, swept_ref, trans_ref, cross0)
 
     lane = lax.broadcasted_iota(jnp.int32, (1, n), 1)
     glob = [(owner_ref[b] * ncols + lane // per_dev) * rows_dev + rows_ref[b : b + 1, :] for b in range(2)]
-    diag = lax.broadcasted_iota(jnp.int32, (n, n), 0) == lax.broadcasted_iota(jnp.int32, (n, n), 1)
     here = first + lax.broadcasted_iota(jnp.int32, (rows_dev, 1), 0)
     sub = lax.broadcasted_iota(jnp.int32, (n, 1), 0)
     there = (owner_ref[1] * ncols + sub // per_dev) * rows_dev + rows_col_ref[:, 1:2]
 
     def decay(positions, b):
         dist = jnp.abs(positions - glob[b]).astype(jnp.float32)
-        return jnp.exp(-dist / jnp.float32(local_len))
+        return jnp.exp(-dist / jnp.float32(local_len)) * -scale
 
     def local_mask(b):
         return jnp.where(lane < 128, mask_ref[b, 0, 0], mask_ref[b, 0, 1]).astype(jnp.float32)
-
-    def cross0(i, carry):
-        at = pl.ds(pl.multiple_of(i * 128, 128), 128)
-        t_ref[at, :] = dot_nt(q_ref[at, :], q_ref[obs0:, :]) * scale
-        return carry
-
-    lax.fori_loop(0, q_ref.shape[0] // 128, cross0, 0)
-    c_ref[...] = t_ref[obs0:, :] + jnp.where(diag, var_ref[0:1, :], 0.0)
-    invert_in_place(c_ref)
 
     t_ref[:rows_dev, :] = t_ref[:rows_dev, :] * (decay(here, 0) * local_mask(0))
     for c in range(ncols):
@@ -171,31 +253,64 @@
             [jnp.broadcast_to(kept_ref[c, i : i + 1, :], (per_dev, 128)) for i in range(2)], axis=1
         )
         t_ref[at, :] = t_ref[at, :] * (decay(there[c * per_dev : (c + 1) * per_dev], 0) * kept)
-    innov0 = value_col_ref[:, 0:1] - mean_ref[obs0:, :]
-
-    def update(i, carry):
-        at = pl.ds(pl.multiple_of(i * 128, 128), 128)
-        gain = -dot_nn(t_ref[at, :], c_ref[...])
-        mean_ref[at, :] = mean_ref[at, :] + dot_nn(gain, innov0)
-        q_ref[at, :] = q_ref[at, :] - 0.5 * dot_nn(gain, q_ref[obs0:, :])
-        return carry
-
-    lax.fori_loop(0, obs0 // 128, update, 0)
-
-    def cross1(i, carry):
-        at = pl.ds(pl.multiple_of(i * 128, 128), 128)
-        t_ref[at, :] = dot_nt(q_ref[at, :], q_ref[obs1:obs0, :]) * scale
-        return carry
-
-    lax.fori_loop(0, obs0 // 128, cross1, 0)
-    c_ref[...] = t_ref[obs1:obs0, :] + jnp.where(diag, var_ref[1:2, :], 0.0)
-    invert_in_place(c_ref)
-    innov1 = value_col_ref[:, 1:2] - mean_ref[obs1:obs0, :]
-    tapered = t_ref[:rows_dev, :] * (decay(here, 1) * local_mask(1))
-    gain = -dot_nn(tapered, c_ref[...])
-    mean = mean_ref[:rows_dev, :] + dot_nn(gain, innov1)
-    change = dot_nn(gain, q_ref[obs1:obs0, :])
-    out_ref[...] = mean[:, 0:1] + q_ref[:rows_dev, :] - 0.5 * change
+    for p, part in enumerate(split(c_ref[...], 3)):
+        v_ref[p] = part
+
+    def gain(at, parts):
+        return split(dot_parts(split(t_ref[at, :], 3), [v_ref[i] for i in range(3)], 0), parts)
+
+    def gain0(i, carry):
+        at = chunk(i, 128)
+        for p, part in enumerate(gain(at, 3)):
+            g_ref[p, at, :] = part
+        return carry
+
+    lax.fori_loop(0, obs0 // 128, gain0, 0)
+    for p, part in enumerate(split(value_col_ref[:, 0:1] - mean_ref[obs0:, :], 3)):
+        innov_ref[p] = part
+
+    c_ref[...] = jnp.where(diag, var_ref[1:2, :], 0.0)
+
+    def covariance1(j, carry):
+        at = chunk(j, wide)
+        change = dot_parts(
+            [g_ref[i, obs1:obs0, :] for i in range(3)], [s0_ref[i, :, at] for i in range(3)], 0
+        )
+        parts = split(q_ref[obs1:obs0, at] - 0.5 * change, 3)
+        for i in range(3):
+            s1_ref[i, :, at] = parts[i]
+        c_ref[...] += dot_parts(parts, parts, 1) * scale
+        return carry
+
+    lax.fori_loop(0, members // wide, covariance1, 0)
+    t_ref[:rows_dev, :] = jnp.zeros((rows_dev, n), jnp.float32)
+
+    def cross1(j):
+        at = chunk(j, 128)
+        some = chunk(j, obs0 // (members // 128))
+        mean_ref[some, :] += dot_parts(
+            [g_ref[i, some, :] for i in range(3)], [innov_ref[i] for i in range(3)], 0
+        )
+        change = dot_parts(
+            [g_ref[i, :rows_dev, :] for i in range(2)], [s0_ref[i, :, at] for i in range(2)], 0
+        )
+        anom = q_ref[:rows_dev, at] - 0.5 * change
+        q_ref[:rows_dev, at] = anom
+        t_ref[:rows_dev, :] += dot_parts(
+            split(anom, 3), [s1_ref[i, :, at] for i in range(3)], 1
+        )
+
+    invert_in_place(c_ref, panel_ref, swept_ref, trans_ref, cross1)
+    innov1 = split(value_col_ref[:, 1:2] - mean_ref[obs1:obs0, :], 2)
+    t_ref[:rows_dev, :] = t_ref[:rows_dev, :] * (decay(here, 1) * local_mask(1))
+    for p, part in enumerate(split(c_ref[...], 3)):
+        v_ref[p] = part
+    gain1 = gain(slice(0, rows_dev), 2)
+    mean = mean_ref[:rows_dev, :] + dot_parts(gain1, innov1, 0)
+    for j in range(members // wide):
+        at = slice(j * wide, (j + 1) * wide)
+        change = dot_parts(gain1, [s1_ref[i, :, at] for i in range(2)], 0)
+        out_ref[:, at] = jnp.concatenate([mean] * 2, axis=1) + q_ref[:rows_dev, at] - 0.5 * change
 
 
 def to_all(x, axis, copies, groups=None):
@@ -227,10 +342,17 @@
         out_specs=pl.BlockSpec(memory_space=VMEM),
         scratch_shapes=[
             VMEM((total, members), jnp.float32),
-            VMEM((total, n), jnp.float32),
+            VMEM((3, n, members), jnp.bfloat16),
+            VMEM((3, n, members), jnp.bfloat16),
+            VMEM((rows_dev + n, n), jnp.float32),
             VMEM((n, n), jnp.float32),
-            VMEM((8, 128), jnp.float32),
+            VMEM((3, rows_dev + n, n), jnp.bfloat16),
             VMEM((total, 128), jnp.float32),
+            VMEM((PIVOTS, n), jnp.float32),
+            VMEM((2, PIVOTS, n), jnp.float32),
+            VMEM((2, n, len(TERMS) * PIVOTS), jnp.bfloat16),
+            VMEM((3, n, n), jnp.bfloat16),
+            VMEM((3, n, 128), jnp.bfloat16),
         ],
         compiler_params=pltpu.CompilerParams(vmem_limit_bytes=40 * 1024 * 1024),
         name="assimilate",

time: 110 us -> 98 us (0.89)
  Pallas kernels: 38.7 us -> 26.7 us
    pallas_call x1, Pallas kernels: 36.9 us -> 24.8 us  [assimilate(): pl.pallas_call(functools.partial(assimilate_kernel, ncols=ncols, local_le...]
where the time goes in v2:
time: 98 us; the launch traced here: 97.5 us
  blocking collectives  42.3 us (43%)
  Pallas kernels  26.7 us (27%)
  starting transfers between devices  16.4 us (17%)
  waiting for transfers between devices  4.64 us (5%)
  between operations  3.72 us (4%)
  local copies, waits for them, and re-layouts  3.67 us (4%)
    all_to_all x2, blocking collectives, to_all(): lax.all_to_all(wide, axis, split_axis=0, concat_axis=0, axis_index_groups...  42.3 us
    pallas_call x1, Pallas kernels, assimilate(): pl.pallas_call(functools.partial(assimilate_kernel, ncols=ncols, local_le...  24.8 us
    all_to_all x1, starting transfers between devices, gather_observed(): lax.all_to_all(picked, 'row', split_axis=0, concat_axis=0, tiled=True)  10.4 us
    ppermute x1, starting transfers between devices, gather_observed(): other = lax.ppermute(own, 'row', [(r, r ^ 1) for r in range(nrows)])  6.05 us
    all_to_all x1, waiting for transfers between devices, gather_observed(): lax.all_to_all(picked, 'row', split_axis=0, concat_axis=0, tiled=True)  4.12 us
    unnamed x14, local copies, waits for them, and re-layouts  2.95 us
  transfers between devices with their start and end apart: 2, of which 2 were waited for; matrix products, arithmetic and copies ran while one was open for 1% of the time, Pallas kernels for 0%

profile of v2, /device:TPU:1, one launch (start us, length us, event | category | flops | bytes accessed | tf_op | source)
XLA Modules:
  0.0 97.5 jit_solution(5715589976564955467)
XLA Ops:
  0.0 1.9 %pick_rows.1 = f32[32,16,128]{2,1,0:T(8,128)} custom-call(s32[2,256]{1,0:T(2,128)} %rows_ref.3, s32[1]{0:T(128)} %bitcast.2.col_ref, s32[2,1,2]{2,1,0:T(1,128)} %mask_ref.3, f32[128,1024]{1,0:T(8,128)} %x_ref.3), custom_call_target="tpu_custom_call" | custom-call | tf_op jit(solution)/shard_map/pick_rows/pallas_call | solution.py:324
  1.9 10.4 %all-to-all-start = ((f32[32,16,128]{2,1,0:T(8,128)}), f32[32,16,128]{2,1,0:T(8,128)S(1)}, u32[]{:S(2)}, u32[]{:S(2)}) async-start(f32[32,16,128]{2,1,0:T(8,128)} %pick_rows.1), calls=%async_computation | async-start | bytes 524288 | tf_op jit(solution)/shard_map/all_to_all | solution.py:365
  12.3 0.0 copy-start.2
  12.3 0.6 copy-done.2
  12.9 0.6 fusion.1
  17.1 4.1 %all-to-all-done = f32[32,16,128]{2,1,0:T(8,128)S(1)} async-done(((f32[32,16,128]{2,1,0:T(8,128)}), f32[32,16,128]{2,1,0:T(8,128)S(1)}, u32[]{:S(2)}, u32[]{:S(2)}) %all-to-all-start) | async-done | bytes 262176 | tf_op jit(solution)/shard_map/all_to_all | solution.py:365
  21.3 24.9 %all_to_all.15 = f32[16,16,128]{2,1,0:T(8,128)S(1)} all-to-all(f32[16,16,128]{2,1,0:T(8,128)S(1)} %broadcast_in_dim.7), channel_id=1, replica_groups=mesh['row'=32,'col'=16] {'col'}, dimensions={0} | all-to-all | bytes 262144 | tf_op jit(solution)/shard_map/all_to_all | solution.py:318
  46.2 0.1 broadcast_in_dim.8
  46.3 0.0 copy-start
  46.3 17.3 %all_to_all.16.own_ref = f32[16,16,8,128]{3,2,1,0:T(8,128)S(1)} all-to-all(f32[16,16,8,128]{3,2,1,0:T(8,128)S(1)} %broadcast_in_dim.8), channel_id=1, replica_groups={{0,32,64,96,128,160,192,224,256,288,320,352,384,416,448,480},{16,48,80,..., dimensions={0} | all-to-all | bytes 2097152 | tf_op jit(solution)/shard_map/all_to_all | solution.py:318
  63.7 6.1 %collective-permute-start = (f32[16,16,8,128]{3,2,1,0:T(8,128)S(1)}, f32[16,16,8,128]{3,2,1,0:T(8,128)S(1)}, u32[]{:S(2)}, u32[]{:S(2)}) collective-permute-start(f32[16,16,8,128]{3,2,1,0:T(8,128)S(1)} %all_to_all.16.own_ref), channel_id=1, source_target_pairs={{0,16},{16,0},{32,48},{48,32},{64,80},{80,64},{96,112},{112,96},{1... | collective-permute-start | bytes 3145736 | tf_op jit(solution)/shard_map/ppermute | solution.py:373
  69.7 0.0 copy-start.1
  69.7 0.7 copy-done.1
  70.4 0.1 copy.7
  70.6 0.0 copy-start.5
  70.6 0.7 copy-done.5
  71.2 0.1 copy.8
  71.4 0.1 pad_add_fusion.place_ref
  71.5 0.5 collective-permute-done.other_ref
  72.0 0.0 copy-start.4
  72.0 0.0 copy-start.3
  72.0 0.0 copy-done
  72.0 0.7 copy-done.4
  72.7 0.0 copy-done.3
  72.7 24.8 %assimilate.1 = f32[128,1024]{1,0:T(8,128)} custom-call(s32[2]{0:T(128)S(1)} %pad_add_fusion.place_ref, s32[2]{0:T(128)S(1)} %copy-done.2, s32[2,1,2]{2,1,0:T(1,128)S(1)} %copy-done.3, f32[128,1024]{1,0:T(8,128)S(1)} %copy-done, f32[16,16,8,128]{3,2,1,0:T(8,128)S(1)} %all_to_all.16.own_ref, f32[16,16,8,128]{3,2,1,0:T(8,128)S(1)} %collective-permute-done.other_ref, ...), custom_call_target="tpu_custom_call" | custom-call | tf_op jit(solution)/shard_map/assimilate/pallas_call | solution.py:338
  (4 shorter events, 0.0 us)
Async XLA Ops:
  1.9 19.4 %all-to-all-start = ((f32[32,16,128]{2,1,0:T(8,128)}), f32[32,16,128]{2,1,0:T(8,128)S(1)}, u32[]{:S(2)}, u32[]{:S(2)}) async-start(f32[32,16,128]{2,1,0:T(8,128)} %pick_rows.1), calls=%async_computation | async-start | bytes 524288 | tf_op jit(solution)/shard_map/all_to_all | solution.py:365
  12.3 0.7 copy-start.2
  46.3 25.7 %copy-start = (f32[128,1024]{1,0:T(8,128)S(1)}, f32[128,1024]{1,0:T(8,128)}, u32[]{:S(2)}) copy-start(f32[128,1024]{1,0:T(8,128)} %x_ref.3) | copy-start | bytes 1572868
  63.7 8.3 %collective-permute-start = (f32[16,16,8,128]{3,2,1,0:T(8,128)S(1)}, f32[16,16,8,128]{3,2,1,0:T(8,128)S(1)}, u32[]{:S(2)}, u32[]{:S(2)}) collective-permute-start(f32[16,16,8,128]{3,2,1,0:T(8,128)S(1)} %all_to_all.16.own_ref), channel_id=1, source_target_pairs={{0,16},{16,0},{32,48},{48,32},{64,80},{80,64},{96,112},{112,96},{1... | collective-permute-start | bytes 3145736 | tf_op jit(solution)/shard_map/ppermute | solution.py:373
  69.7 0.7 copy-start.1
  70.6 0.7 copy-start.5
  72.0 0.7 copy-start.4
  72.0 0.7 copy-start.3

commit v3 on v2

v3 whole, which is shorter than its diff:
```python
import functools

import jax
import jax.numpy as jnp
from jax import lax
from jax.experimental import pallas as pl
from jax.experimental.pallas import tpu as pltpu
from jax.sharding import PartitionSpec as P

VMEM = pltpu.VMEM
SMEM = pltpu.SMEM
PIVOTS = 32
TERMS = ((0, 0), (0, 1), (1, 0), (1, 1), (0, 2), (2, 0))


def split(x, parts):
    out = []
    for i in range(parts):
        out.append(x.astype(jnp.bfloat16))
        if i < parts - 1:
            x = x - out[-1].astype(jnp.float32)
    return out


def dot_parts(a, b, contract):
    pairs = TERMS[: 3 if len(a) == 2 else 6]
    left = jnp.concatenate([a[i] for i, _ in pairs], axis=1)
    right = jnp.concatenate([b[j] for _, j in pairs], axis=contract)
    return lax.dot_general(
        left, right, (((1,), (contract,)), ((), ())), preferred_element_type=jnp.float32
    )


def by_terms(x, side):
    parts = split(x, 3)
    return jnp.concatenate([parts[term[side]] for term in TERMS], axis=0)


def one_pass(a, b):
    return jnp.dot(a, b, preferred_element_type=jnp.float32)


def spread(x, row):
    return jnp.broadcast_to(x[row : row + 1, :], (8, 128))


def sweep_panel(panel, base, lanes, subs):
    high = base >= 128
    q0 = base - jnp.where(high, 128, 0)
    low_half = [panel[8 * g : 8 * g + 8, :128] for g in range(4)]
    high_half = [panel[8 * g : 8 * g + 8, 128:] for g in range(4)]
    act = [jnp.where(high, h, l) for l, h in zip(low_half, high_half)]
    oth = [jnp.where(high, l, h) for l, h in zip(low_half, high_half)]

    def column(g, c):
        return jnp.take_along_axis(act[g], jnp.full((8, 128), q0 + c, jnp.int32), axis=1)

    diag = [column(0, l) for l in range(8)]
    for sb in range(4):
        cols = [[None] * 4 for _ in range(8)]
        later = [g for g in range(sb + 1, 4)] + [g for g in range(sb)]
        for g in later[:1]:
            for l in range(8):
                cols[l][g] = column(g, 8 * sb + l)
        following = [column(sb + 1, 8 * sb + 8 + l) for l in range(8)] if sb < 3 else None
        for g in later[1:]:
            for l in range(8):
                cols[l][g] = column(g, 8 * sb + l)
        invs, factors = [], [[None] * 8 for _ in range(8)]
        for l in range(8):
            at_row = subs == l
            inv = 1.0 / spread(diag[l], l)
            invs.append(inv)
            for m in range(l + 1, 8):
                t = spread(diag[m], l) * inv
                factors[l][m] = t
                diag[m] = jnp.where(at_row, t, diag[m] - diag[l] * t)
        for l in range(8):
            cols[l][sb] = diag[l]
        for g in later:
            for l in range(8):
                for m in range(l + 1, 8):
                    cols[m][g] = cols[m][g] - cols[l][g] * factors[l][m]
        if sb < 3:
            for l in range(8):
                scaled = cols[l][sb + 1] * invs[l]
                following = [f - cols[l][sb + 1] * spread(scaled, m) for m, f in enumerate(following)]
        for l in range(8):
            u = cols[l]
            at_row = subs == l
            at_lane = lanes == q0 + (8 * sb + l)
            inv = invs[l]
            row_act = jnp.where(at_lane, -inv, spread(act[sb], l) * inv)
            row_oth = spread(oth[sb], l) * inv
            act = [jnp.where(at_lane, 0.0, act[g]) - u[g] * row_act for g in range(4)]
            oth = [oth[g] - u[g] * row_oth for g in range(4)]
            act[sb] = jnp.where(at_row, row_act, act[sb])
            oth[sb] = jnp.where(at_row, row_oth, oth[sb])
        diag = following
    act, oth = jnp.concatenate(act, 0), jnp.concatenate(oth, 0)
    return jnp.concatenate(
        [jnp.where(high, oth, act), jnp.where(high, act, oth)], axis=1
    )


def invert_in_place(a_ref, panel_ref, swept_ref, trans_ref, beside):
    n = a_ref.shape[0]
    steps = n // PIVOTS
    lanes = lax.broadcasted_iota(jnp.int32, (8, 128), 1)
    subs = lax.broadcasted_iota(jnp.int32, (8, 128), 0)
    columns = lax.broadcasted_iota(jnp.int32, (n, n), 1)

    def inside(k, rows):
        return (columns[:rows] >= k * PIVOTS) & (columns[:rows] < (k + 1) * PIVOTS)

    def rows_of(k):
        return pl.ds(pl.multiple_of(k * PIVOTS, PIVOTS), PIVOTS)

    def apply(k, slot):
        a_ref[...] = jnp.where(inside(k, n), 0.0, a_ref[...]) - one_pass(
            trans_ref[slot], by_terms(swept_ref[slot], 1)
        )

    panel_ref[...] = a_ref[:PIVOTS, :]
    swept_ref[1] = jnp.zeros_like(panel_ref)
    trans_ref[1] = jnp.zeros(trans_ref.shape[1:], jnp.bfloat16)

    def step(k, carry):
        now, before = k % 2, (k + 1) % 2
        panel = panel_ref[...]
        trans_ref[now] = by_terms(panel, 0).T
        swept = sweep_panel(panel, k * PIVOTS, lanes, subs)
        apply(k - 1, before)
        last = jnp.maximum(k - 1, 0)
        a_ref[rows_of(last), :] = jnp.where(k > 0, swept_ref[before], a_ref[rows_of(last), :])
        beside(k)
        following = jnp.minimum(k + 1, steps - 1)
        panel_ref[...] = jnp.where(inside(k, PIVOTS), 0.0, a_ref[rows_of(following), :]) - one_pass(
            trans_ref[now, rows_of(following), :], by_terms(swept, 1)
        )
        swept_ref[now] = swept
        return carry

    lax.fori_loop(0, steps, step, 0)
    final = (steps - 1) % 2
    apply(steps - 1, final)
    a_ref[n - PIVOTS :, :] = swept_ref[final]


def pick_kernel(rows_ref, col_ref, mask_ref, x_ref, out_ref, held):
    members = x_ref.shape[1]
    per_dev = held.shape[0] // 2
    start = col_ref[0] * per_dev
    for b in range(2):
        for i in range(per_dev):
            r = rows_ref[b, start + i]
            held[b * per_dev + i : b * per_dev + i + 1, :] = x_ref[pl.ds(r, 1), :]
    chunks = members // 128
    lanes = lax.broadcasted_iota(jnp.int32, (1, 128), 1)
    kept = jnp.where(lanes == 0, mask_ref[0, 0, 0], mask_ref[0, 0, 1]).astype(jnp.float32)
    for piece in range(out_ref.shape[0]):
        g, j = piece // chunks, piece % chunks
        for s in range(8):
            out_ref[piece, :, 128 * s : 128 * s + 128] = held[8 * g + s : 8 * g + s + 1, 128 * j : 128 * j + 128]
        out_ref[piece, :, 1024:] = kept


def forward_kernel(source_ref, pieces_ref, out_ref):
    for s in range(9):
        at = slice(128 * s, 128 * s + 128)
        line = pieces_ref[source_ref[0 if s < 8 else 1], :, at]
        for d in range(out_ref.shape[0]):
            out_ref[d, :, at] = line


def share_kernel(line_ref, out_ref, kept_ref, held):
    for c in range(line_ref.shape[0]):
        for s in range(8):
            held[c, s : s + 1, :] = line_ref[c, :, 128 * s : 128 * s + 128]
        kept_ref[c : c + 1, :] = line_ref[c, :, 1024:]
    for d in range(out_ref.shape[0]):
        out_ref[d] = held[...]


def prepare_kernel(
    place_ref, owner_ref, mask_ref, x_ref, rows_ref, rows_col_ref, value_col_ref, var_ref,
    rho_ref, decay_ref, anom_ref, mean_ref, value_ref, held_var_ref, *, ncols, local_len,
):
    rows_dev, members = x_ref.shape
    n = rows_ref.shape[1]
    per_dev = n // ncols
    lane = lax.broadcasted_iota(jnp.int32, (1, n), 1)
    here = place_ref[1] + lax.broadcasted_iota(jnp.int32, (rows_dev, 1), 0)
    sub = lax.broadcasted_iota(jnp.int32, (n, 1), 0)
    there = (owner_ref[1] * ncols + sub // per_dev) * rows_dev + rows_col_ref[:, 1:2]

    def decay(positions, b):
        glob = (owner_ref[b] * ncols + lane // per_dev) * rows_dev + rows_ref[b : b + 1, :]
        dist = jnp.abs(positions - glob).astype(jnp.float32)
        return jnp.exp(-dist / jnp.float32(local_len))

    for b in range(2):
        mask = jnp.where(lane < 128, mask_ref[b, 0, 0], mask_ref[b, 0, 1]).astype(jnp.float32)
        rho_ref[b] = decay(here, b) * mask
    decay_ref[...] = decay(there, 0)
    x = x_ref[...]
    mean = jnp.sum(x, axis=1, keepdims=True) * (1.0 / members)
    anom_ref[...] = x - mean
    mean_ref[...] = jnp.broadcast_to(mean, mean_ref.shape)
    held = lax.broadcasted_iota(jnp.int32, value_ref.shape, 1)
    value_ref[...] = jnp.where(held == 0, value_col_ref[:, 0:1], value_col_ref[:, 1:2])
    held_var_ref[...] = var_ref[...]


def assimilate_kernel(
    place_ref, own_ref, other_ref, kept_ref, rho_ref, decay_ref, x_ref, x_mean_ref, value_ref, var_ref,
    out_ref, q_ref, s0_ref, s1_ref, t_ref, c_ref, g_ref, mean_ref, panel_ref, swept_ref, trans_ref,
    v_ref, innov_ref, stage_ref, sems,
):
    rows_dev, members = x_ref.shape
    n = var_ref.shape[1]
    ncols = kept_ref.shape[0]
    per_dev = n // ncols
    groups = per_dev // 8
    chunks = members // 128
    core = place_ref[0]
    scale = 1.0 / (members - 1.0)
    obs1, obs0 = rows_dev, rows_dev + n

    def member_chunk(i, side):
        return pl.ds(pl.multiple_of((2 * i + (core if side == 0 else 1 - core)) * 128, 128), 128)

    def chunk(j, width):
        return pl.ds(pl.multiple_of(j * width, width), width)

    def observed(b, i, ref):
        return jnp.concatenate(
            [ref[(b * groups + g) * (chunks // 2) + i, c] for c in range(ncols) for g in range(groups)], axis=0
        )

    def add_up(c, carry):
        for b, top in ((0, obs0), (1, obs1)):
            for g in range(groups):
                slots = [(b * groups + g) * (chunks // 2) + i for i in range(chunks // 2)]
                total = own_ref[slots[0], c] + other_ref[slots[0], c]
                for slot in slots[1:]:
                    total = total + (own_ref[slot, c] + other_ref[slot, c])
                mean_ref[pl.ds(pl.multiple_of(top + c * per_dev + g * 8, 8), 8), :] = total
        return carry

    lax.fori_loop(0, ncols, add_up, 0)
    mean = jnp.sum(mean_ref[obs1:, :], axis=1, keepdims=True) * (1.0 / members)
    mean_ref[obs1:, :] = jnp.broadcast_to(mean, (2 * n, 128))
    mean_ref[:rows_dev, :] = x_mean_ref[...]

    wide = 2 * 128
    diag = lax.broadcasted_iota(jnp.int32, (n, n), 0) == lax.broadcasted_iota(jnp.int32, (n, n), 1)
    c_ref[...] = jnp.where(diag, var_ref[0:1, :], 0.0)

    def covariance0(i, carry):
        mean = mean_ref[obs0:, :]
        anom = jnp.concatenate([observed(0, i, own_ref) - mean, observed(0, i, other_ref) - mean], axis=1)
        parts = split(anom, 3)
        for p in range(3):
            s0_ref[p, :, chunk(i, wide)] = parts[p]
        c_ref[...] += dot_parts(parts, parts, 1) * scale
        return carry

    lax.fori_loop(0, members // wide, covariance0, 0)
    t_ref[...] = jnp.zeros_like(t_ref)

    def cross0(j):
        at, i, side = chunk(j, 128), j // 2, j % 2
        local = jnp.where(side == 0, x_ref[:, member_chunk(i, 0)], x_ref[:, member_chunk(i, 1)])
        seen = jnp.where(side == 0, observed(1, i, own_ref), observed(1, i, other_ref))
        for top, anom in ((0, local), (obs1, seen - mean_ref[obs1:obs0, :])):
            rows = slice(top, top + anom.shape[0])
            q_ref[rows, at] = anom
            t_ref[rows, :] += dot_parts(split(anom, 3), [s0_ref[p, :, at] for p in range(3)], 1)

    invert_in_place(c_ref, panel_ref, swept_ref, trans_ref, cross0)

    t_ref[:rows_dev, :] = t_ref[:rows_dev, :] * (rho_ref[0] * -scale)
    for c in range(ncols):
        at = slice(obs1 + c * per_dev, obs1 + (c + 1) * per_dev)
        kept = jnp.concatenate(
            [jnp.broadcast_to(kept_ref[c : c + 1, i : i + 1] * -scale, (per_dev, 128)) for i in range(2)], axis=1
        )
        t_ref[at, :] = t_ref[at, :] * (decay_ref[c * per_dev : (c + 1) * per_dev, :] * kept)
    for p, part in enumerate(split(c_ref[...], 3)):
        v_ref[p] = part

    def gain(at, parts):
        return split(dot_parts(split(t_ref[at, :], 3), [v_ref[p] for p in range(3)], 0), parts)

    def gain0(i, carry):
        at = chunk(i, 128)
        for p, part in enumerate(gain(at, 3)):
            g_ref[p, at, :] = part
        return carry

    lax.fori_loop(0, obs0 // 128, gain0, 0)
    for p, part in enumerate(split(value_ref[:, 0:1] - mean_ref[obs0:, :], 3)):
        innov_ref[p] = part

    c_ref[...] = jnp.where(diag, var_ref[1:2, :], 0.0)

    def covariance1(i, carry):
        at = chunk(i, wide)
        change = dot_parts(
            [g_ref[p, obs1:obs0, :] for p in range(3)], [s0_ref[p, :, at] for p in range(3)], 0
        )
        parts = split(q_ref[obs1:obs0, at] - 0.5 * change, 3)
        for p in range(3):
            s1_ref[p, :, at] = parts[p]
        c_ref[...] += dot_parts(parts, parts, 1) * scale
        return carry

    lax.fori_loop(0, members // wide, covariance1, 0)
    t_ref[:rows_dev, :] = jnp.zeros((rows_dev, n), jnp.float32)

    def cross1(j):
        at = chunk(j, 128)
        some = chunk(j, obs0 // chunks)
        mean_ref[some, :] += dot_parts(
            [g_ref[p, some, :] for p in range(3)], [innov_ref[p] for p in range(3)], 0
        )
        change = dot_parts(
            [g_ref[p, :rows_dev, :] for p in range(2)], [s0_ref[p, :, at] for p in range(2)], 0
        )
        anom = q_ref[:rows_dev, at] - 0.5 * change
        q_ref[:rows_dev, at] = anom
        t_ref[:rows_dev, :] += dot_parts(split(anom, 3), [s1_ref[p, :, at] for p in range(3)], 1)

    invert_in_place(c_ref, panel_ref, swept_ref, trans_ref, cross1)
    innov1 = split(value_ref[:, 1:2] - mean_ref[obs1:obs0, :], 2)
    t_ref[:rows_dev, :] = t_ref[:rows_dev, :] * (rho_ref[1] * -scale)
    for p, part in enumerate(split(c_ref[...], 3)):
        v_ref[p] = part
    gain1 = gain(slice(0, rows_dev), 2)
    mean = mean_ref[:rows_dev, :] + dot_parts(gain1, innov1, 0)
    copies = []
    for i in range(members // wide):
        at = slice(i * wide, (i + 1) * wide)
        change = dot_parts(gain1, [s1_ref[p, :, at] for p in range(2)], 0)
        stage_ref[:, at] = jnp.concatenate([mean] * 2, axis=1) + q_ref[:rows_dev, at] - 0.5 * change
        for side in range(2):
            j = 2 * i + side
            copies.append(
                pltpu.make_async_copy(
                    stage_ref.at[:, 128 * j : 128 * j + 128], out_ref.at[:, member_chunk(i, side)], sems.at[j]
                )
            )
            copies[-1].start()
    for copy in copies:
        copy.wait()


def on_core(kernel, name, outs, smem, vmem, scratch=(), limit_mib=6):
    return pl.pallas_call(
        kernel,
        out_shape=outs,
        in_specs=[pl.BlockSpec(memory_space=SMEM)] * len(smem) + [pl.BlockSpec(memory_space=VMEM)] * len(vmem),
        out_specs=jax.tree.map(lambda _: pl.BlockSpec(memory_space=VMEM), outs),
        scratch_shapes=list(scratch),
        compiler_params=pltpu.CompilerParams(vmem_limit_bytes=limit_mib and limit_mib * 1024 * 1024),
        name=name,
    )(*smem, *vmem)


def exchange(x, axis, groups=None):
    return lax.all_to_all(x, axis, split_axis=0, concat_axis=0, axis_index_groups=groups, tiled=True)


def floats(*shape):
    return jax.ShapeDtypeStruct(shape, jnp.float32)


def prepare(place, owner, taper_mask, ensemble, obs_rows, obs_value, obs_var, ncols, local_len):
    rows_dev, members = ensemble.shape
    n = obs_rows.shape[1]
    return on_core(
        functools.partial(prepare_kernel, ncols=ncols, local_len=local_len), "prepare",
        (floats(2, rows_dev, n), floats(n, n), floats(rows_dev, members), floats(rows_dev, 128),
         floats(n, 128), floats(2, n)),
        (place, owner, taper_mask), (ensemble, obs_rows, obs_rows.T, obs_value.T, obs_var),
    )


def assimilate(place, own, other, kept, prepared):
    rows_dev, members = prepared[2].shape
    n = prepared[1].shape[0]
    total = rows_dev + 2 * n
    return pl.pallas_call(
        assimilate_kernel,
        out_shape=floats(rows_dev, members),
        in_specs=[pl.BlockSpec(memory_space=SMEM)] + [pl.BlockSpec(memory_space=VMEM)] * (3 + len(prepared)),
        out_specs=pl.BlockSpec(memory_space=pl.ANY),
        scratch_shapes=[
            VMEM((rows_dev + n, members), jnp.float32),
            VMEM((3, n, members), jnp.bfloat16),
            VMEM((3, n, members), jnp.bfloat16),
            VMEM((rows_dev + n, n), jnp.float32),
            VMEM((n, n), jnp.float32),
            VMEM((3, rows_dev + n, n), jnp.bfloat16),
            VMEM((total, 128), jnp.float32),
            VMEM((PIVOTS, n), jnp.float32),
            VMEM((2, PIVOTS, n), jnp.float32),
            VMEM((2, n, len(TERMS) * PIVOTS), jnp.bfloat16),
            VMEM((3, n, n), jnp.bfloat16),
            VMEM((3, n, 128), jnp.bfloat16),
            VMEM((rows_dev, members), jnp.float32),
            pltpu.SemaphoreType.DMA((members // 128,)),
        ],
        compiler_params=pltpu.CompilerParams(vmem_limit_bytes=40 * 1024 * 1024),
        name="assimilate",
    )(place, own, other, kept, *prepared)


def on_device(ensemble, obs_rows, owner, obs_value, obs_var, taper_mask):
    rows, members = ensemble.shape
    ncols, nrows = lax.axis_size("col"), lax.axis_size("row")
    my_row, my_col = lax.axis_index("row"), lax.axis_index("col")
    per_dev = obs_rows.shape[1] // ncols
    picked = on_core(
        pick_kernel, "pick_rows", floats(nrows, 1, 1024 + 128),
        (obs_rows, my_col[None], taper_mask), (ensemble,), [VMEM((2 * per_dev, members), jnp.float32)], None,
    )
    pieces = exchange(picked, "row")
    place = jnp.stack([my_row % 2, (my_row * ncols + my_col) * rows]).astype(jnp.int32)
    source = jnp.stack([jnp.where(my_row < nrows // 2, owner[0], owner[1]), owner[1]])
    prepared = prepare(place, owner, taper_mask, ensemble, obs_rows, obs_value, obs_var, ncols, rows * nrows * ncols // 4)
    pieces, source, place, *prepared = lax.optimization_barrier((pieces, source, place, *prepared))
    line = exchange(on_core(forward_kernel, "forward", floats(ncols, 1, 1024 + 128), (source,), (pieces,)), "col")
    wide, kept = on_core(
        share_kernel, "share", (floats(nrows // 2, ncols, 8, 128), floats(ncols, 128)),
        (), (line,), [VMEM((ncols, 8, 128), jnp.float32)],
    )
    own = exchange(wide, "row", [[r for r in range(nrows) if r % 2 == c] for c in range(2)])
    other = lax.ppermute(own, "row", [(r, r ^ 1) for r in range(nrows)])
    return assimilate(place, own, other, kept, prepared)


def solution(mesh):
    in_specs = (P(("row", "col"), None), P(), P(), P(), P(), P(None, ("row", "col"), None))
    out_specs = P(("row", "col"), None)
    return jax.shard_map(
        on_device, mesh=mesh, in_specs=in_specs, out_specs=out_specs, check_vma=False
    )
```

time: 98 us -> 96.9 us (0.989)
  between operations: 3.72 us -> 1.29 us
  blocking collectives: 42.3 us -> 44.5 us
  starting transfers between devices: 16.4 us -> 15.3 us
    all_to_all x2, blocking collectives: 42.3 us -> 44.5 us  [exchange(): lax.all_to_all(x, axis, split_axis=0, concat_axis=0, axis_index_groups=gr...]
    all_to_all x1, waiting for transfers between devices: 4.12 us -> 2.23 us  [exchange(): lax.all_to_all(x, axis, split_axis=0, concat_axis=0, axis_index_groups=gr...]
    ppermute x1, waiting for transfers between devices: 0.52 us -> 2.26 us  [on_device(): other = lax.ppermute(own, 'row', [(r, r ^ 1) for r in range(nrows)])]
    ppermute x1, starting transfers between devices: 6.05 us -> 4.8 us  [on_device(): other = lax.ppermute(own, 'row', [(r, r ^ 1) for r in range(nrows)])]
    pallas_call x2 -> x5, Pallas kernels: 26.7 us -> 27.4 us  [the longest x1 24 us: assimilate(): pl.pallas_call(assimilate_kernel, out_shape=floats(rows_dev, members), in...]
  transfers between devices with their start and end apart: 2 -> 2, of which waited for: 2 -> 2; matrix products, arithmetic and copies ran while one was open for 1% -> 2% of each run, Pallas kernels for 0% -> 1%
where the time goes in v3:
time: 96.9 us; the launch traced here: 96.6 us
  blocking collectives  44.5 us (46%)
  Pallas kernels  27.4 us (28%)
  starting transfers between devices  15.3 us (16%)
  waiting for transfers between devices  4.5 us (5%)
  local copies, waits for them, and re-layouts  2.9 us (3%)
  between operations  1.29 us (1%)
    all_to_all x2, blocking collectives, exchange(): lax.all_to_all(x, axis, split_axis=0, concat_axis=0, axis_index_groups=gr...  44.5 us
    pallas_call x1, Pallas kernels, assimilate(): pl.pallas_call(assimilate_kernel, out_shape=floats(rows_dev, members), in...  24 us
    all_to_all x1, starting transfers between devices, exchange(): lax.all_to_all(x, axis, split_axis=0, concat_axis=0, axis_index_groups=gr...  10.5 us
    ppermute x1, starting transfers between devices, on_device(): other = lax.ppermute(own, 'row', [(r, r ^ 1) for r in range(nrows)])  4.8 us
    pallas_call x4, Pallas kernels, on_core(): pl.pallas_call(kernel, out_shape=outs, in_specs=[pl.BlockSpec(memory_spac...  3.46 us
    unnamed x14, local copies, waits for them, and re-layouts  2.32 us
    ppermute x1, waiting for transfers between devices, on_device(): other = lax.ppermute(own, 'row', [(r, r ^ 1) for r in range(nrows)])  2.26 us
    all_to_all x1, waiting for transfers between devices, exchange(): lax.all_to_all(x, axis, split_axis=0, concat_axis=0, axis_index_groups=gr...  2.23 us
  transfers between devices with their start and end apart: 2, of which 2 were waited for; matrix products, arithmetic and copies ran while one was open for 2% of the time, Pallas kernels for 1%

profile of v3, /device:TPU:1, one launch (start us, length us, event | category | flops | bytes accessed | tf_op | source)
XLA Modules:
  0.0 96.6 jit_solution(7644495607583644097)
XLA Ops:
  0.0 0.0 copy-start
  0.0 2.0 %pick_rows.1 = f32[32,1,1152]{2,1,0:T(1,128)} custom-call(s32[2,256]{1,0:T(2,128)} %rows_ref.3, s32[1]{0:T(128)} %bitcast.col_ref, s32[2,1,2]{2,1,0:T(1,128)} %mask_ref.3, f32[128,1024]{1,0:T(8,128)} %x_ref.3), custom_call_target="tpu_custom_call" | custom-call | tf_op jit(solution)/shard_map/pick_rows/pallas_call | solution.py:360
  2.0 0.0 copy-start.2
  2.0 10.5 %all-to-all-start = ((f32[32,1,1152]{2,1,0:T(1,128)}), f32[32,1,1152]{2,1,0:T(1,128)S(1)}, u32[]{:S(2)}, u32[]{:S(2)}) async-start(f32[32,1,1152]{2,1,0:T(1,128)} %pick_rows.1), calls=%async_computation | async-start | bytes 294912 | tf_op jit(solution)/shard_map/all_to_all | solution.py:372
  12.5 0.0 copy-done.2
  12.5 0.6 fusion
  13.0 0.0 copy-start.1
  13.0 0.7 copy-done.1
  13.7 0.1 copy.7
  13.9 0.0 copy-start.5
  13.9 0.7 copy-done.5
  14.6 0.1 copy.8
  15.9 0.6 pad_add_fusion
  16.5 0.0 copy-start.4
  16.5 0.0 copy-start.3
  16.5 0.0 copy-done
  16.6 0.7 copy-done.4
  17.2 0.0 copy-done.3
  17.2 0.8 prepare.1
  18.1 2.2 %all-to-all-done.pieces_ref = f32[32,1,1152]{2,1,0:T(1,128)S(1)} async-done(((f32[32,1,1152]{2,1,0:T(1,128)}), f32[32,1,1152]{2,1,0:T(1,128)S(1)}, u32[]{:S(2)}, u32[]{:S(2)}) %all-to-all-start) | async-done | bytes 147488 | tf_op jit(solution)/shard_map/all_to_all | solution.py:372
  20.3 0.6 forward.1
  20.9 24.6 %all_to_all.15.line_ref = f32[16,1,1152]{2,1,0:T(1,128)S(1)} all-to-all(f32[16,1,1152]{2,1,0:T(1,128)S(1)} %forward.1), channel_id=1, replica_groups=mesh['row'=32,'col'=16] {'col'}, dimensions={0} | all-to-all | bytes 147456 | tf_op jit(solution)/shard_map/all_to_all | solution.py:372
  45.5 0.1 share.1
  45.6 19.9 %all_to_all.16.own_ref = f32[16,16,8,128]{3,2,1,0:T(8,128)S(1)} all-to-all(f32[16,16,8,128]{3,2,1,0:T(8,128)S(1)} %get-tuple-element.31), channel_id=1, replica_groups={{0,32,64,96,128,160,192,224,256,288,320,352,384,416,448,480},{16,48,80,..., dimensions={0} | all-to-all | bytes 2097152 | tf_op jit(solution)/shard_map/all_to_all | solution.py:372
  65.5 4.8 %collective-permute-start = (f32[16,16,8,128]{3,2,1,0:T(8,128)S(1)}, f32[16,16,8,128]{3,2,1,0:T(8,128)S(1)}, u32[]{:S(2)}, u32[]{:S(2)}) collective-permute-start(f32[16,16,8,128]{3,2,1,0:T(8,128)S(1)} %all_to_all.16.own_ref), channel_id=1, source_target_pairs={{0,16},{16,0},{32,48},{48,32},{64,80},{80,64},{96,112},{112,96},{1... | collective-permute-start | bytes 3145736 | tf_op jit(solution)/shard_map/ppermute | solution.py:440
  70.3 2.3 %collective-permute-done.other_ref = f32[16,16,8,128]{3,2,1,0:T(8,128)S(1)} collective-permute-done((f32[16,16,8,128]{3,2,1,0:T(8,128)S(1)}, f32[16,16,8,128]{3,2,1,0:T(8,128)S(1)}, u32[]{:S(2)}, u32[]{:S(2)}) %collective-permute-start) | collective-permute-done | bytes 1048608 | tf_op jit(solution)/shard_map/ppermute | solution.py:440
  72.6 24.0 %assimilate.1 = f32[128,1024]{1,0:T(8,128)} custom-call(s32[2]{0:T(128)S(1)} %get-tuple-element.28.place_ref, f32[16,16,8,128]{3,2,1,0:T(8,128)S(1)} %all_to_all.16.own_ref, f32[16,16,8,128]{3,2,1,0:T(8,128)S(1)} %collective-permute-done.other_ref, f32[16,128]{1,0:T(8,128)S(1)} %get-tuple-element.32.kept_ref, f32[2,128,256]{2,1,0:T(8,128)S(1)} %get-tuple-element.33.rho_ref, ...), custom_call_target="tpu_custom_call" | custom-call | tf_op jit(solution)/shard_map/assimilate/pallas_call | solution.py:394
Async XLA Ops:
  0.0 16.5 %copy-start = (f32[128,1024]{1,0:T(8,128)S(1)}, f32[128,1024]{1,0:T(8,128)}, u32[]{:S(2)}) copy-start(f32[128,1024]{1,0:T(8,128)} %x_ref.3) | copy-start | bytes 1572868
  2.0 10.5 %copy-start.2 = (s32[2]{0:T(128)S(1)}, s32[2]{0:T(128)}, u32[]{:S(2)}) copy-start(s32[2]{0:T(128)} %owner_ref.1) | copy-start | bytes 28
  2.0 18.4 %all-to-all-start = ((f32[32,1,1152]{2,1,0:T(1,128)}), f32[32,1,1152]{2,1,0:T(1,128)S(1)}, u32[]{:S(2)}, u32[]{:S(2)}) async-start(f32[32,1,1152]{2,1,0:T(1,128)} %pick_rows.1), calls=%async_computation | async-start | bytes 294912 | tf_op jit(solution)/shard_map/all_to_all | solution.py:372
  13.0 0.7 copy-start.1
  13.9 0.7 copy-start.5
  16.5 0.7 copy-start.4
  16.5 0.7 copy-start.3
  65.5 7.1 %collective-permute-start = (f32[16,16,8,128]{3,2,1,0:T(8,128)S(1)}, f32[16,16,8,128]{3,2,1,0:T(8,128)S(1)}, u32[]{:S(2)}, u32[]{:S(2)}) collective-permute-start(f32[16,16,8,128]{3,2,1,0:T(8,128)S(1)} %all_to_all.16.own_ref), channel_id=1, source_target_pairs={{0,16},{16,0},{32,48},{48,32},{64,80},{80,64},{96,112},{112,96},{1... | collective-permute-start | bytes 3145736 | tf_op jit(solution)/shard_map/ppermute | solution.py:440

commit v4 on v3

--- a/solution.py
+++ b/solution.py
@@ -165,14 +165,6 @@
         out_ref[piece, :, 1024:] = kept
 
 
-def forward_kernel(source_ref, pieces_ref, out_ref):
-    for s in range(9):
-        at = slice(128 * s, 128 * s + 128)
-        line = pieces_ref[source_ref[0 if s < 8 else 1], :, at]
-        for d in range(out_ref.shape[0]):
-            out_ref[d, :, at] = line
-
-
 def share_kernel(line_ref, out_ref, kept_ref, held):
     for c in range(line_ref.shape[0]):
         for s in range(8):
@@ -183,16 +175,22 @@
 
 
 def prepare_kernel(
-    place_ref, owner_ref, mask_ref, x_ref, rows_ref, rows_col_ref, value_col_ref, var_ref,
+    first_ref, owner_ref, mask_ref, x_ref, rows_ref, given_ref, var_ref,
     rho_ref, decay_ref, anom_ref, mean_ref, value_ref, held_var_ref, *, ncols, local_len,
 ):
     rows_dev, members = x_ref.shape
     n = rows_ref.shape[1]
     per_dev = n // ncols
     lane = lax.broadcasted_iota(jnp.int32, (1, n), 1)
-    here = place_ref[1] + lax.broadcasted_iota(jnp.int32, (rows_dev, 1), 0)
+    here = first_ref[0] + lax.broadcasted_iota(jnp.int32, (rows_dev, 1), 0)
     sub = lax.broadcasted_iota(jnp.int32, (n, 1), 0)
-    there = (owner_ref[1] * ncols + sub // per_dev) * rows_dev + rows_col_ref[:, 1:2]
+    diag = lax.broadcasted_iota(jnp.int32, (n, n), 0) == lax.broadcasted_iota(jnp.int32, (n, n), 1)
+
+    def column(row):
+        return jnp.sum(jnp.where(diag, row, 0.0), axis=1, keepdims=True)
+
+    seen = column(rows_ref[1:2, :].astype(jnp.float32)).astype(jnp.int32)
+    there = (owner_ref[1] * ncols + sub // per_dev) * rows_dev + seen
 
     def decay(positions, b):
         glob = (owner_ref[b] * ncols + lane // per_dev) * rows_dev + rows_ref[b : b + 1, :]
@@ -208,14 +206,14 @@
     anom_ref[...] = x - mean
     mean_ref[...] = jnp.broadcast_to(mean, mean_ref.shape)
     held = lax.broadcasted_iota(jnp.int32, value_ref.shape, 1)
-    value_ref[...] = jnp.where(held == 0, value_col_ref[:, 0:1], value_col_ref[:, 1:2])
+    value_ref[...] = jnp.where(held == 0, column(given_ref[0:1, :]), column(given_ref[1:2, :]))
     held_var_ref[...] = var_ref[...]
 
 
 def assimilate_kernel(
-    place_ref, own_ref, other_ref, kept_ref, rho_ref, decay_ref, x_ref, x_mean_ref, value_ref, var_ref,
+    core_ref, own_ref, other_ref, kept_ref, rho_ref, decay_ref, x_ref, x_mean_ref, value_ref, var_ref,
     out_ref, q_ref, s0_ref, s1_ref, t_ref, c_ref, g_ref, mean_ref, panel_ref, swept_ref, trans_ref,
-    v_ref, innov_ref, stage_ref, sems,
+    v_ref, innov_ref, w_ref, v1_ref, e_ref, stage_ref, sems,
 ):
     rows_dev, members = x_ref.shape
     n = var_ref.shape[1]
@@ -223,7 +221,7 @@
     per_dev = n // ncols
     groups = per_dev // 8
     chunks = members // 128
-    core = place_ref[0]
+    core = core_ref[0]
     scale = 1.0 / (members - 1.0)
     obs1, obs0 = rows_dev, rows_dev + n
 
@@ -255,7 +253,7 @@
 
     wide = 2 * 128
     diag = lax.broadcasted_iota(jnp.int32, (n, n), 0) == lax.broadcasted_iota(jnp.int32, (n, n), 1)
-    c_ref[...] = jnp.where(diag, var_ref[0:1, :], 0.0)
+    c_ref[...] = jnp.zeros_like(c_ref)
 
     def covariance0(i, carry):
         mean = mean_ref[obs0:, :]
@@ -263,11 +261,15 @@
         parts = split(anom, 3)
         for p in range(3):
             s0_ref[p, :, chunk(i, wide)] = parts[p]
-        c_ref[...] += dot_parts(parts, parts, 1) * scale
+        c_ref[...] += dot_parts(parts, parts, 1)
         return carry
 
     lax.fori_loop(0, members // wide, covariance0, 0)
+    for p, part in enumerate(split(c_ref[...], 3)):
+        w_ref[p] = part
+    c_ref[...] = c_ref[...] * scale + jnp.where(diag, var_ref[0:1, :], 0.0)
     t_ref[...] = jnp.zeros_like(t_ref)
+    e_ref[...] = jnp.zeros_like(e_ref)
 
     def cross0(j):
         at, i, side = chunk(j, 128), j // 2, j % 2
@@ -276,68 +278,81 @@
         for top, anom in ((0, local), (obs1, seen - mean_ref[obs1:obs0, :])):
             rows = slice(top, top + anom.shape[0])
             q_ref[rows, at] = anom
-            t_ref[rows, :] += dot_parts(split(anom, 3), [s0_ref[p, :, at] for p in range(3)], 1)
+            parts = split(anom, 3)
+            t_ref[rows, :] += dot_parts(parts, [s0_ref[p, :, at] for p in range(3)], 1)
+            if top:
+                e_ref[...] += dot_parts(parts, parts, 1)
 
     invert_in_place(c_ref, panel_ref, swept_ref, trans_ref, cross0)
 
-    t_ref[:rows_dev, :] = t_ref[:rows_dev, :] * (rho_ref[0] * -scale)
-    for c in range(ncols):
-        at = slice(obs1 + c * per_dev, obs1 + (c + 1) * per_dev)
-        kept = jnp.concatenate(
-            [jnp.broadcast_to(kept_ref[c : c + 1, i : i + 1] * -scale, (per_dev, 128)) for i in range(2)], axis=1
-        )
-        t_ref[at, :] = t_ref[at, :] * (decay_ref[c * per_dev : (c + 1) * per_dev, :] * kept)
     for p, part in enumerate(split(c_ref[...], 3)):
         v_ref[p] = part
 
-    def gain(at, parts):
-        return split(dot_parts(split(t_ref[at, :], 3), [v_ref[p] for p in range(3)], 0), parts)
-
-    def gain0(i, carry):
-        at = chunk(i, 128)
-        for p, part in enumerate(gain(at, 3)):
+    def gain(tapered, parts):
+        return split(dot_parts(split(tapered, 3), [v_ref[p] for p in range(3)], 0), parts)
+
+    for half in range(2):
+        kept = jnp.concatenate(
+            [
+                jnp.concatenate(
+                    [jnp.broadcast_to(kept_ref[c : c + 1, i : i + 1] * -scale, (per_dev, 128)) for i in range(2)],
+                    axis=1,
+                )
+                for c in range(half * ncols // 2, (half + 1) * ncols // 2)
+            ],
+            axis=0,
+        )
+        rows = slice(half * n // 2, (half + 1) * n // 2)
+        at = slice(obs1 + half * n // 2, obs1 + (half + 1) * n // 2)
+        for p, part in enumerate(gain(t_ref[at, :] * (decay_ref[rows, :] * kept), 3)):
             g_ref[p, at, :] = part
-        return carry
-
-    lax.fori_loop(0, obs0 // 128, gain0, 0)
+
+    for half in range(2):
+        at = slice(obs1 + half * n // 2, obs1 + (half + 1) * n // 2)
+        product = dot_parts([g_ref[p, at, :] for p in range(3)], [w_ref[p] for p in range(3)], 0)
+        for p, part in enumerate(split(0.25 * product - t_ref[at, :], 3)):
+            v1_ref[p, half * n // 2 : (half + 1) * n // 2, :] = part
+    for half in range(2):
+        at = slice(obs1 + half * n // 2, obs1 + (half + 1) * n // 2)
+        c_ref[half * n // 2 : (half + 1) * n // 2, :] = dot_parts(
+            [g_ref[p, at, :] for p in range(3)], [v1_ref[p] for p in range(3)], 1
+        )
+    c_ref[...] = (e_ref[...] + 0.5 * (c_ref[...] + c_ref[...].T)) * scale + jnp.where(diag, var_ref[1:2, :], 0.0)
+
+    for p, part in enumerate(gain(t_ref[:rows_dev, :] * (rho_ref[0] * -scale), 2)):
+        g_ref[p, :rows_dev, :] = part
     for p, part in enumerate(split(value_ref[:, 0:1] - mean_ref[obs0:, :], 3)):
         innov_ref[p] = part
-
-    c_ref[...] = jnp.where(diag, var_ref[1:2, :], 0.0)
-
-    def covariance1(i, carry):
-        at = chunk(i, wide)
+    t_ref[:rows_dev, :] = jnp.zeros((rows_dev, n), jnp.float32)
+
+    def cross1(j):
+        at = chunk(j, 128)
+        some = pl.ds(pl.multiple_of(obs1 + j * (n // chunks), n // chunks), n // chunks)
+        mean_ref[some, :] += dot_parts(
+            [g_ref[p, some, :] for p in range(3)], [innov_ref[p] for p in range(3)], 0
+        )
+        some = chunk(j, rows_dev // chunks)
+        mean_ref[some, :] += dot_parts(
+            [g_ref[p, some, :] for p in range(2)], [innov_ref[p] for p in range(2)], 0
+        )
         change = dot_parts(
             [g_ref[p, obs1:obs0, :] for p in range(3)], [s0_ref[p, :, at] for p in range(3)], 0
         )
-        parts = split(q_ref[obs1:obs0, at] - 0.5 * change, 3)
+        seen = split(q_ref[obs1:obs0, at] - 0.5 * change, 3)
         for p in range(3):
-            s1_ref[p, :, at] = parts[p]
-        c_ref[...] += dot_parts(parts, parts, 1) * scale
-        return carry
-
-    lax.fori_loop(0, members // wide, covariance1, 0)
-    t_ref[:rows_dev, :] = jnp.zeros((rows_dev, n), jnp.float32)
-
-    def cross1(j):
-        at = chunk(j, 128)
-        some = chunk(j, obs0 // chunks)
-        mean_ref[some, :] += dot_parts(
-            [g_ref[p, some, :] for p in range(3)], [innov_ref[p] for p in range(3)], 0
-        )
+            s1_ref[p, :, at] = seen[p]
         change = dot_parts(
             [g_ref[p, :rows_dev, :] for p in range(2)], [s0_ref[p, :, at] for p in range(2)], 0
         )
         anom = q_ref[:rows_dev, at] - 0.5 * change
         q_ref[:rows_dev, at] = anom
-        t_ref[:rows_dev, :] += dot_parts(split(anom, 3), [s1_ref[p, :, at] for p in range(3)], 1)
+        t_ref[:rows_dev, :] += dot_parts(split(anom, 3), seen, 1)
 
     invert_in_place(c_ref, panel_ref, swept_ref, trans_ref, cross1)
     innov1 = split(value_ref[:, 1:2] - mean_ref[obs1:obs0, :], 2)
-    t_ref[:rows_dev, :] = t_ref[:rows_dev, :] * (rho_ref[1] * -scale)
     for p, part in enumerate(split(c_ref[...], 3)):
         v_ref[p] = part
-    gain1 = gain(slice(0, rows_dev), 2)
+    gain1 = gain(t_ref[:rows_dev, :] * (rho_ref[1] * -scale), 2)
     mean = mean_ref[:rows_dev, :] + dot_parts(gain1, innov1, 0)
     copies = []
     for i in range(members // wide):
@@ -376,18 +391,18 @@
     return jax.ShapeDtypeStruct(shape, jnp.float32)
 
 
-def prepare(place, owner, taper_mask, ensemble, obs_rows, obs_value, obs_var, ncols, local_len):
+def prepare(first, owner, taper_mask, ensemble, obs_rows, obs_value, obs_var, ncols, local_len):
     rows_dev, members = ensemble.shape
     n = obs_rows.shape[1]
     return on_core(
         functools.partial(prepare_kernel, ncols=ncols, local_len=local_len), "prepare",
         (floats(2, rows_dev, n), floats(n, n), floats(rows_dev, members), floats(rows_dev, 128),
          floats(n, 128), floats(2, n)),
-        (place, owner, taper_mask), (ensemble, obs_rows, obs_rows.T, obs_value.T, obs_var),
-    )
-
-
-def assimilate(place, own, other, kept, prepared):
+        (first, owner, taper_mask), (ensemble, obs_rows, obs_value, obs_var), limit_mib=None,
+    )
+
+
+def assimilate(core, own, other, kept, prepared):
     rows_dev, members = prepared[2].shape
     n = prepared[1].shape[0]
     total = rows_dev + 2 * n
@@ -409,12 +424,15 @@
             VMEM((2, n, len(TERMS) * PIVOTS), jnp.bfloat16),
             VMEM((3, n, n), jnp.bfloat16),
             VMEM((3, n, 128), jnp.bfloat16),
+            VMEM((3, n, n), jnp.bfloat16),
+            VMEM((3, n, n), jnp.bfloat16),
+            VMEM((n, n), jnp.float32),
             VMEM((rows_dev, members), jnp.float32),
             pltpu.SemaphoreType.DMA((members // 128,)),
         ],
         compiler_params=pltpu.CompilerParams(vmem_limit_bytes=40 * 1024 * 1024),
         name="assimilate",
-    )(place, own, other, kept, *prepared)
+    )(core, own, other, kept, *prepared)
 
 
 def on_device(ensemble, obs_rows, owner, obs_value, obs_var, taper_mask):
@@ -427,18 +445,21 @@
         (obs_rows, my_col[None], taper_mask), (ensemble,), [VMEM((2 * per_dev, members), jnp.float32)], None,
     )
     pieces = exchange(picked, "row")
-    place = jnp.stack([my_row % 2, (my_row * ncols + my_col) * rows]).astype(jnp.int32)
-    source = jnp.stack([jnp.where(my_row < nrows // 2, owner[0], owner[1]), owner[1]])
-    prepared = prepare(place, owner, taper_mask, ensemble, obs_rows, obs_value, obs_var, ncols, rows * nrows * ncols // 4)
-    pieces, source, place, *prepared = lax.optimization_barrier((pieces, source, place, *prepared))
-    line = exchange(on_core(forward_kernel, "forward", floats(ncols, 1, 1024 + 128), (source,), (pieces,)), "col")
+    first, core = ((my_row * ncols + my_col) * rows)[None], (my_row & 1)[None]
+    prepared = prepare(first, owner, taper_mask, ensemble, obs_rows, obs_value, obs_var, ncols, rows * nrows * ncols // 4)
+    source = jnp.where(my_row < nrows // 2, owner[0], owner[1])
+    source, seen, pieces, *prepared = lax.optimization_barrier((source, owner[1], pieces, *prepared))
+    tile = lax.dynamic_index_in_dim(pieces, source, 0)[:, :, :1024]
+    mask = lax.dynamic_index_in_dim(pieces, seen, 0)[:, :, 1024:]
+    line = jnp.broadcast_to(jnp.concatenate([tile, mask], axis=2), (ncols, 1, 1024 + 128))
+    line = exchange(line, "col")
     wide, kept = on_core(
         share_kernel, "share", (floats(nrows // 2, ncols, 8, 128), floats(ncols, 128)),
         (), (line,), [VMEM((ncols, 8, 128), jnp.float32)],
     )
     own = exchange(wide, "row", [[r for r in range(nrows) if r % 2 == c] for c in range(2)])
     other = lax.ppermute(own, "row", [(r, r ^ 1) for r in range(nrows)])
-    return assimilate(place, own, other, kept, prepared)
+    return assimilate(core, own, other, kept, prepared)
 
 
 def solution(mesh):

time: 96.9 us -> 94.2 us (0.972)
  Pallas kernels: 27.4 us -> 25.2 us
  between operations: 1.29 us -> 3.05 us
  local copies, waits for them, and re-layouts: 2.9 us -> 1.32 us
    pallas_call x1, Pallas kernels: 24 us -> 20.9 us  [assimilate(): pl.pallas_call(assimilate_kernel, out_shape=floats(rows_dev, members), in...]
    unnamed x14, local copies, waits for them, and re-layouts: 2.32 us -> 0.68 us
    pallas_call x4 -> x3, Pallas kernels: 3.46 us -> 4.29 us  [on_core(): pl.pallas_call(kernel, out_shape=outs, in_specs=[pl.BlockSpec(memory_spac...]
  transfers between devices with their start and end apart: 2 -> 2, of which waited for: 2 -> 2; matrix products, arithmetic and copies ran while one was open for 2% -> 1% of each run, Pallas kernels for 1% -> 2%
where the time goes in v4:
time: 94.2 us; the launch traced here: 93.8 us
  blocking collectives  43.8 us (46%)
  Pallas kernels  25.2 us (27%)
  starting transfers between devices  15.2 us (16%)
  waiting for transfers between devices  5.32 us (6%)
  between operations  3.05 us (3%)
  local copies, waits for them, and re-layouts  1.32 us (1%)
    all_to_all x2, blocking collectives, exchange(): lax.all_to_all(x, axis, split_axis=0, concat_axis=0, axis_index_groups=gr...  43.8 us
    pallas_call x1, Pallas kernels, assimilate(): pl.pallas_call(assimilate_kernel, out_shape=floats(rows_dev, members), in...  20.9 us
    all_to_all x1, starting transfers between devices, exchange(): lax.all_to_all(x, axis, split_axis=0, concat_axis=0, axis_index_groups=gr...  10.3 us
    ppermute x1, starting transfers between devices, on_device(): other = lax.ppermute(own, 'row', [(r, r ^ 1) for r in range(nrows)])  4.8 us
    pallas_call x3, Pallas kernels, on_core(): pl.pallas_call(kernel, out_shape=outs, in_specs=[pl.BlockSpec(memory_spac...  4.29 us
    all_to_all x1, waiting for transfers between devices, exchange(): lax.all_to_all(x, axis, split_axis=0, concat_axis=0, axis_index_groups=gr...  3.07 us
    ppermute x1, waiting for transfers between devices, on_device(): other = lax.ppermute(own, 'row', [(r, r ^ 1) for r in range(nrows)])  2.25 us
  transfers between devices with their start and end apart: 2, of which 2 were waited for; matrix products, arithmetic and copies ran while one was open for 1% of the time, Pallas kernels for 2%

profile of v4, /device:TPU:1, one launch (start us, length us, event | category | flops | bytes accessed | tf_op | source)
XLA Modules:
  0.0 93.8 jit_solution(17164081721228067647)
XLA Ops:
  0.0 1.9 %pick_rows.1 = f32[32,1,1152]{2,1,0:T(1,128)} custom-call(s32[2,256]{1,0:T(2,128)} %rows_ref.3, s32[1]{0:T(128)} %bitcast.3.col_ref, s32[2,1,2]{2,1,0:T(1,128)} %mask_ref.3, f32[128,1024]{1,0:T(8,128)} %x_ref.3), custom_call_target="tpu_custom_call" | custom-call | tf_op jit(solution)/shard_map/pick_rows/pallas_call | solution.py:375
  1.9 10.3 %all-to-all-start = ((f32[32,1,1152]{2,1,0:T(1,128)}), f32[32,1,1152]{2,1,0:T(1,128)S(1)}, u32[]{:S(2)}, u32[]{:S(2)}) async-start(f32[32,1,1152]{2,1,0:T(1,128)} %pick_rows.1), calls=%async_computation | async-start | bytes 294912 | tf_op jit(solution)/shard_map/all_to_all | solution.py:387
  12.2 0.0 copy-start.6
  12.3 0.6 copy-done.6
  12.9 0.6 fusion
  14.7 2.3 %prepare.1 = (f32[2,128,256]{2,1,0:T(8,128)}, f32[256,256]{1,0:T(8,128)}, f32[128,1024]{1,0:T(8,128)}, f32[128,128]{1,0:T(8,128)}, f32[256,128]{1,0:T(8,128)}, /*index=5*/f32[2,256]{1,0:T(2,128)}) custom-call(s32[1]{0:T(128)} %bitcast.4.first_ref, s32[2]{0:T(128)} %owner_ref.1, s32[2,1,2]{2,1,0:T(1,128)} %mask_ref.3, f32[128,1024]{1,0:T(8,128)} %x_ref.3, ...), custom_call_target="tpu_custom_call" | custom-call | tf_op jit(solution)/shard_map/prepare/pallas_call | solution.py:375
  17.0 3.1 %all-to-all-done = f32[32,1,1152]{2,1,0:T(1,128)S(1)} async-done(((f32[32,1,1152]{2,1,0:T(1,128)}), f32[32,1,1152]{2,1,0:T(1,128)S(1)}, u32[]{:S(2)}, u32[]{:S(2)}) %all-to-all-start) | async-done | bytes 147488 | tf_op jit(solution)/shard_map/all_to_all | solution.py:387
  21.9 24.6 %all_to_all.15.line_ref = f32[16,1,1152]{2,1,0:T(1,128)S(1)} all-to-all(f32[16,1,1152]{2,1,0:T(1,128)S(1)} %broadcast_in_dim.20), channel_id=1, replica_groups=mesh['row'=32,'col'=16] {'col'}, dimensions={0} | all-to-all | bytes 147456 | tf_op jit(solution)/shard_map/all_to_all | solution.py:387
  46.5 0.1 share.1
  46.5 0.0 copy-start
  46.6 0.0 copy-start.1
  46.6 0.0 copy-start.2
  46.6 0.0 copy-start.3
  46.6 0.0 copy-start.4
  46.6 19.2 %all_to_all.16.own_ref = f32[16,16,8,128]{3,2,1,0:T(8,128)S(1)} all-to-all(f32[16,16,8,128]{3,2,1,0:T(8,128)S(1)} %get-tuple-element.31), channel_id=1, replica_groups={{0,32,64,96,128,160,192,224,256,288,320,352,384,416,448,480},{16,48,80,..., dimensions={0} | all-to-all | bytes 2097152 | tf_op jit(solution)/shard_map/all_to_all | solution.py:387
  65.8 4.8 %collective-permute-start = (f32[16,16,8,128]{3,2,1,0:T(8,128)S(1)}, f32[16,16,8,128]{3,2,1,0:T(8,128)S(1)}, u32[]{:S(2)}, u32[]{:S(2)}) collective-permute-start(f32[16,16,8,128]{3,2,1,0:T(8,128)S(1)} %all_to_all.16.own_ref), channel_id=1, source_target_pairs={{0,16},{16,0},{32,48},{48,32},{64,80},{80,64},{96,112},{112,96},{1... | collective-permute-start | bytes 3145736 | tf_op jit(solution)/shard_map/ppermute | solution.py:461
  70.6 0.0 copy-start.5
  70.7 2.3 %collective-permute-done.other_ref = f32[16,16,8,128]{3,2,1,0:T(8,128)S(1)} collective-permute-done((f32[16,16,8,128]{3,2,1,0:T(8,128)S(1)}, f32[16,16,8,128]{3,2,1,0:T(8,128)S(1)}, u32[]{:S(2)}, u32[]{:S(2)}) %collective-permute-start) | collective-permute-done | bytes 1048608 | tf_op jit(solution)/shard_map/ppermute | solution.py:461
  72.9 0.0 copy-done
  72.9 0.0 copy-done.1
  72.9 0.0 copy-done.2
  72.9 0.0 copy-done.3
  72.9 0.0 copy-done.4
  72.9 0.0 copy-done.5
  72.9 20.9 %assimilate.1 = f32[128,1024]{1,0:T(8,128)} custom-call(s32[1]{0:T(128)} %bitcast.core_ref, f32[16,16,8,128]{3,2,1,0:T(8,128)S(1)} %all_to_all.16.own_ref, f32[16,16,8,128]{3,2,1,0:T(8,128)S(1)} %collective-permute-done.other_ref, f32[16,128]{1,0:T(8,128)S(1)} %get-tuple-element.32.kept_ref, f32[2,128,256]{2,1,0:T(8,128)S(1)} %copy-done.1, ...), custom_call_target="tpu_custom_call" | custom-call | tf_op jit(solution)/shard_map/assimilate/pallas_call | solution.py:409
  (4 shorter events, 0.1 us)
Async XLA Ops:
  1.9 18.2 %all-to-all-start = ((f32[32,1,1152]{2,1,0:T(1,128)}), f32[32,1,1152]{2,1,0:T(1,128)S(1)}, u32[]{:S(2)}, u32[]{:S(2)}) async-start(f32[32,1,1152]{2,1,0:T(1,128)} %pick_rows.1), calls=%async_computation | async-start | bytes 294912 | tf_op jit(solution)/shard_map/all_to_all | solution.py:387
  12.2 0.7 copy-start.6
  46.5 26.4 %copy-start = (f32[128,1024]{1,0:T(8,128)S(1)}, f32[128,1024]{1,0:T(8,128)}, u32[]{:S(2)}) copy-start(f32[128,1024]{1,0:T(8,128)} %get-tuple-element.35.x_ref) | copy-start | bytes 1572868
  46.6 26.4 %copy-start.1 = (f32[2,128,256]{2,1,0:T(8,128)S(1)}, f32[2,128,256]{2,1,0:T(8,128)}, u32[]{:S(2)}) copy-start(f32[2,128,256]{2,1,0:T(8,128)} %get-tuple-element.33.rho_ref) | copy-start | bytes 786436
  46.6 26.3 %copy-start.2 = (f32[256,256]{1,0:T(8,128)S(1)}, f32[256,256]{1,0:T(8,128)}, u32[]{:S(2)}) copy-start(f32[256,256]{1,0:T(8,128)} %get-tuple-element.34.decay_ref) | copy-start | bytes 786436
  46.6 26.3 %copy-start.3 = (f32[256,128]{1,0:T(8,128)S(1)}, f32[256,128]{1,0:T(8,128)}, u32[]{:S(2)}) copy-start(f32[256,128]{1,0:T(8,128)} %get-tuple-element.37.value_ref) | copy-start | bytes 393220
  46.6 26.3 %copy-start.4 = (f32[128,128]{1,0:T(8,128)S(1)}, f32[128,128]{1,0:T(8,128)}, u32[]{:S(2)}) copy-start(f32[128,128]{1,0:T(8,128)} %get-tuple-element.36.x_mean_ref) | copy-start | bytes 196612
  65.8 7.1 %collective-permute-start = (f32[16,16,8,128]{3,2,1,0:T(8,128)S(1)}, f32[16,16,8,128]{3,2,1,0:T(8,128)S(1)}, u32[]{:S(2)}, u32[]{:S(2)}) collective-permute-start(f32[16,16,8,128]{3,2,1,0:T(8,128)S(1)} %all_to_all.16.own_ref), channel_id=1, source_target_pairs={{0,16},{16,0},{32,48},{48,32},{64,80},{80,64},{96,112},{112,96},{1... | collective-permute-start | bytes 3145736 | tf_op jit(solution)/shard_map/ppermute | solution.py:461
  70.6 2.3 %copy-start.5 = (f32[2,256]{1,0:T(2,128)S(1)}, f32[2,256]{1,0:T(2,128)}, u32[]{:S(2)}) copy-start(f32[2,256]{1,0:T(2,128)} %get-tuple-element.38.var_ref) | copy-start | bytes 6148

commit v5 on v4

--- a/solution.py
+++ b/solution.py
@@ -448,9 +448,9 @@
     first, core = ((my_row * ncols + my_col) * rows)[None], (my_row & 1)[None]
     prepared = prepare(first, owner, taper_mask, ensemble, obs_rows, obs_value, obs_var, ncols, rows * nrows * ncols // 4)
     source = jnp.where(my_row < nrows // 2, owner[0], owner[1])
-    source, seen, pieces, *prepared = lax.optimization_barrier((source, owner[1], pieces, *prepared))
+    pieces, *prepared = lax.optimization_barrier((pieces, *prepared))
     tile = lax.dynamic_index_in_dim(pieces, source, 0)[:, :, :1024]
-    mask = lax.dynamic_index_in_dim(pieces, seen, 0)[:, :, 1024:]
+    mask = lax.dynamic_index_in_dim(pieces, owner[1], 0)[:, :, 1024:]
     line = jnp.broadcast_to(jnp.concatenate([tile, mask], axis=2), (ncols, 1, 1024 + 128))
     line = exchange(line, "col")
     wide, kept = on_core(

time: 94.2 us -> 94.5 us (level)
  blocking collectives: 43.8 us -> 45.8 us
  waiting for transfers between devices: 5.32 us -> 3.33 us
    all_to_all x2, blocking collectives: 43.8 us -> 45.8 us  [exchange(): lax.all_to_all(x, axis, split_axis=0, concat_axis=0, axis_index_groups=gr...]
    all_to_all x1, waiting for transfers between devices: 3.07 us -> 1.08 us  [exchange(): lax.all_to_all(x, axis, split_axis=0, concat_axis=0, axis_index_groups=gr...]
where the time goes in v5:
time: 94.5 us; the launch traced here: 94.1 us
  blocking collectives  45.8 us (48%)
  Pallas kernels  25.2 us (27%)
  starting transfers between devices  15.2 us (16%)
  waiting for transfers between devices  3.33 us (4%)
  between operations  3.31 us (4%)
  local copies, waits for them, and re-layouts  1.32 us (1%)
    all_to_all x2, blocking collectives, exchange(): lax.all_to_all(x, axis, split_axis=0, concat_axis=0, axis_index_groups=gr...  45.8 us
    pallas_call x1, Pallas kernels, assimilate(): pl.pallas_call(assimilate_kernel, out_shape=floats(rows_dev, members), in...  20.9 us
    all_to_all x1, starting transfers between devices, exchange(): lax.all_to_all(x, axis, split_axis=0, concat_axis=0, axis_index_groups=gr...  10.3 us
    ppermute x1, starting transfers between devices, on_device(): other = lax.ppermute(own, 'row', [(r, r ^ 1) for r in range(nrows)])  4.8 us
    pallas_call x3, Pallas kernels, on_core(): pl.pallas_call(kernel, out_shape=outs, in_specs=[pl.BlockSpec(memory_spac...  4.29 us
    ppermute x1, waiting for transfers between devices, on_device(): other = lax.ppermute(own, 'row', [(r, r ^ 1) for r in range(nrows)])  2.25 us
  transfers between devices with their start and end apart: 2, of which 2 were waited for; matrix products, arithmetic and copies ran while one was open for 1% of the time, Pallas kernels for 2%

profile of v5, /device:TPU:1, one launch (start us, length us, event | category | flops | bytes accessed | tf_op | source)
XLA Modules:
  0.0 94.1 jit_solution(13895986199958714378)
XLA Ops:
  0.0 1.9 %pick_rows.1 = f32[32,1,1152]{2,1,0:T(1,128)} custom-call(s32[2,256]{1,0:T(2,128)} %rows_ref.3, s32[1]{0:T(128)} %bitcast.1.col_ref, s32[2,1,2]{2,1,0:T(1,128)} %mask_ref.3, f32[128,1024]{1,0:T(8,128)} %x_ref.3), custom_call_target="tpu_custom_call" | custom-call | tf_op jit(solution)/shard_map/pick_rows/pallas_call | solution.py:375
  1.9 10.3 %all-to-all-start = ((f32[32,1,1152]{2,1,0:T(1,128)}), f32[32,1,1152]{2,1,0:T(1,128)S(1)}, u32[]{:S(2)}, u32[]{:S(2)}) async-start(f32[32,1,1152]{2,1,0:T(1,128)} %pick_rows.1), calls=%async_computation | async-start | bytes 294912 | tf_op jit(solution)/shard_map/all_to_all | solution.py:387
  12.2 0.0 copy-start.6
  12.2 0.6 copy-done.6
  12.9 0.6 fusion
  16.7 2.3 %prepare.1 = (f32[2,128,256]{2,1,0:T(8,128)}, f32[256,256]{1,0:T(8,128)}, f32[128,1024]{1,0:T(8,128)}, f32[128,128]{1,0:T(8,128)}, f32[256,128]{1,0:T(8,128)}, /*index=5*/f32[2,256]{1,0:T(2,128)}) custom-call(s32[1]{0:T(128)} %bitcast.2.first_ref, s32[2]{0:T(128)} %owner_ref.1, s32[2,1,2]{2,1,0:T(1,128)} %mask_ref.3, f32[128,1024]{1,0:T(8,128)} %x_ref.3, ...), custom_call_target="tpu_custom_call" | custom-call | tf_op jit(solution)/shard_map/prepare/pallas_call | solution.py:375
  19.0 1.1 %all-to-all-done = f32[32,1,1152]{2,1,0:T(1,128)S(1)} async-done(((f32[32,1,1152]{2,1,0:T(1,128)}), f32[32,1,1152]{2,1,0:T(1,128)S(1)}, u32[]{:S(2)}, u32[]{:S(2)}) %all-to-all-start) | async-done | bytes 147488 | tf_op jit(solution)/shard_map/all_to_all | solution.py:387
  20.2 24.6 %all_to_all.15.line_ref = f32[16,1,1152]{2,1,0:T(1,128)S(1)} all-to-all(f32[16,1,1152]{2,1,0:T(1,128)S(1)} %broadcast_in_dim.20), channel_id=1, replica_groups=mesh['row'=32,'col'=16] {'col'}, dimensions={0} | all-to-all | bytes 147456 | tf_op jit(solution)/shard_map/all_to_all | solution.py:387
  44.7 0.1 share.1
  44.8 0.0 copy-start
  44.8 0.0 copy-start.1
  44.8 0.0 copy-start.2
  44.9 0.0 copy-start.3
  44.9 0.0 copy-start.4
  44.9 21.3 %all_to_all.16.own_ref = f32[16,16,8,128]{3,2,1,0:T(8,128)S(1)} all-to-all(f32[16,16,8,128]{3,2,1,0:T(8,128)S(1)} %get-tuple-element.27), channel_id=1, replica_groups={{0,32,64,96,128,160,192,224,256,288,320,352,384,416,448,480},{16,48,80,..., dimensions={0} | all-to-all | bytes 2097152 | tf_op jit(solution)/shard_map/all_to_all | solution.py:387
  66.1 4.8 %collective-permute-start = (f32[16,16,8,128]{3,2,1,0:T(8,128)S(1)}, f32[16,16,8,128]{3,2,1,0:T(8,128)S(1)}, u32[]{:S(2)}, u32[]{:S(2)}) collective-permute-start(f32[16,16,8,128]{3,2,1,0:T(8,128)S(1)} %all_to_all.16.own_ref), channel_id=1, source_target_pairs={{0,16},{16,0},{32,48},{48,32},{64,80},{80,64},{96,112},{112,96},{1... | collective-permute-start | bytes 3145736 | tf_op jit(solution)/shard_map/ppermute | solution.py:461
  70.9 0.0 copy-start.5
  71.0 2.3 %collective-permute-done.other_ref = f32[16,16,8,128]{3,2,1,0:T(8,128)S(1)} collective-permute-done((f32[16,16,8,128]{3,2,1,0:T(8,128)S(1)}, f32[16,16,8,128]{3,2,1,0:T(8,128)S(1)}, u32[]{:S(2)}, u32[]{:S(2)}) %collective-permute-start) | collective-permute-done | bytes 1048608 | tf_op jit(solution)/shard_map/ppermute | solution.py:461
  73.2 0.0 copy-done
  73.2 0.0 copy-done.1
  73.2 0.0 copy-done.2
  73.2 0.0 copy-done.3
  73.2 0.0 copy-done.4
  73.2 0.0 copy-done.5
  73.2 20.9 %assimilate.1 = f32[128,1024]{1,0:T(8,128)} custom-call(s32[1]{0:T(128)} %bitcast.core_ref, f32[16,16,8,128]{3,2,1,0:T(8,128)S(1)} %all_to_all.16.own_ref, f32[16,16,8,128]{3,2,1,0:T(8,128)S(1)} %collective-permute-done.other_ref, f32[16,128]{1,0:T(8,128)S(1)} %get-tuple-element.28.kept_ref, f32[2,128,256]{2,1,0:T(8,128)S(1)} %copy-done.1, ...), custom_call_target="tpu_custom_call" | custom-call | tf_op jit(solution)/shard_map/assimilate/pallas_call | solution.py:409
  (4 shorter events, 0.1 us)
Async XLA Ops:
  1.9 18.2 %all-to-all-start = ((f32[32,1,1152]{2,1,0:T(1,128)}), f32[32,1,1152]{2,1,0:T(1,128)S(1)}, u32[]{:S(2)}, u32[]{:S(2)}) async-start(f32[32,1,1152]{2,1,0:T(1,128)} %pick_rows.1), calls=%async_computation | async-start | bytes 294912 | tf_op jit(solution)/shard_map/all_to_all | solution.py:387
  12.2 0.7 copy-start.6
  44.8 28.4 %copy-start = (f32[128,1024]{1,0:T(8,128)S(1)}, f32[128,1024]{1,0:T(8,128)}, u32[]{:S(2)}) copy-start(f32[128,1024]{1,0:T(8,128)} %get-tuple-element.31.x_ref) | copy-start | bytes 1572868
  44.8 28.4 %copy-start.1 = (f32[2,128,256]{2,1,0:T(8,128)S(1)}, f32[2,128,256]{2,1,0:T(8,128)}, u32[]{:S(2)}) copy-start(f32[2,128,256]{2,1,0:T(8,128)} %get-tuple-element.29.rho_ref) | copy-start | bytes 786436
  44.8 28.4 %copy-start.2 = (f32[256,256]{1,0:T(8,128)S(1)}, f32[256,256]{1,0:T(8,128)}, u32[]{:S(2)}) copy-start(f32[256,256]{1,0:T(8,128)} %get-tuple-element.30.decay_ref) | copy-start | bytes 786436
  44.9 28.4 %copy-start.3 = (f32[256,128]{1,0:T(8,128)S(1)}, f32[256,128]{1,0:T(8,128)}, u32[]{:S(2)}) copy-start(f32[256,128]{1,0:T(8,128)} %get-tuple-element.33.value_ref) | copy-start | bytes 393220
  44.9 28.4 %copy-start.4 = (f32[128,128]{1,0:T(8,128)S(1)}, f32[128,128]{1,0:T(8,128)}, u32[]{:S(2)}) copy-start(f32[128,128]{1,0:T(8,128)} %get-tuple-element.32.x_mean_ref) | copy-start | bytes 196612
  66.1 7.1 %collective-permute-start = (f32[16,16,8,128]{3,2,1,0:T(8,128)S(1)}, f32[16,16,8,128]{3,2,1,0:T(8,128)S(1)}, u32[]{:S(2)}, u32[]{:S(2)}) collective-permute-start(f32[16,16,8,128]{3,2,1,0:T(8,128)S(1)} %all_to_all.16.own_ref), channel_id=1, source_target_pairs={{0,16},{16,0},{32,48},{48,32},{64,80},{80,64},{96,112},{112,96},{1... | collective-permute-start | bytes 3145736 | tf_op jit(solution)/shard_map/ppermute | solution.py:461
  70.9 2.3 %copy-start.5 = (f32[2,256]{1,0:T(2,128)S(1)}, f32[2,256]{1,0:T(2,128)}, u32[]{:S(2)}) copy-start(f32[2,256]{1,0:T(2,128)} %get-tuple-element.34.var_ref) | copy-start | bytes 6148

commit v6 on v5

--- a/solution.py
+++ b/solution.py
@@ -129,11 +129,11 @@
         now, before = k % 2, (k + 1) % 2
         panel = panel_ref[...]
         trans_ref[now] = by_terms(panel, 0).T
+        beside(k)
         swept = sweep_panel(panel, k * PIVOTS, lanes, subs)
         apply(k - 1, before)
         last = jnp.maximum(k - 1, 0)
         a_ref[rows_of(last), :] = jnp.where(k > 0, swept_ref[before], a_ref[rows_of(last), :])
-        beside(k)
         following = jnp.minimum(k + 1, steps - 1)
         panel_ref[...] = jnp.where(inside(k, PIVOTS), 0.0, a_ref[rows_of(following), :]) - one_pass(
             trans_ref[now, rows_of(following), :], by_terms(swept, 1)
@@ -147,10 +147,10 @@
     a_ref[n - PIVOTS :, :] = swept_ref[final]
 
 
-def pick_kernel(rows_ref, col_ref, mask_ref, x_ref, out_ref, held):
+def pick_kernel(rows_ref, mask_ref, x_ref, out_ref, held):
     members = x_ref.shape[1]
     per_dev = held.shape[0] // 2
-    start = col_ref[0] * per_dev
+    start = lax.axis_index("col") * per_dev
     for b in range(2):
         for i in range(per_dev):
             r = rows_ref[b, start + i]
@@ -175,14 +175,18 @@
 
 
 def prepare_kernel(
-    first_ref, owner_ref, mask_ref, x_ref, rows_ref, given_ref, var_ref,
-    rho_ref, decay_ref, anom_ref, mean_ref, value_ref, held_var_ref, *, ncols, local_len,
+    owner_ref, mask_ref, x_ref, rows_ref, given_ref, var_ref,
+    wanted_ref, rho_ref, decay_ref, anom_ref, mean_ref, value_ref, held_var_ref, *, nrows, ncols, local_len,
 ):
     rows_dev, members = x_ref.shape
     n = rows_ref.shape[1]
     per_dev = n // ncols
+    place = lax.broadcasted_iota(jnp.int32, wanted_ref.shape, 1)
+    early = lax.axis_index("row") < nrows // 2
+    wanted_ref[...] = jnp.where((place < 1024) & early, owner_ref[0], owner_ref[1])
     lane = lax.broadcasted_iota(jnp.int32, (1, n), 1)
-    here = first_ref[0] + lax.broadcasted_iota(jnp.int32, (rows_dev, 1), 0)
+    first = (lax.axis_index("row") * ncols + lax.axis_index("col")) * rows_dev
+    here = first + lax.broadcasted_iota(jnp.int32, (rows_dev, 1), 0)
     sub = lax.broadcasted_iota(jnp.int32, (n, 1), 0)
     diag = lax.broadcasted_iota(jnp.int32, (n, n), 0) == lax.broadcasted_iota(jnp.int32, (n, n), 1)
 
@@ -211,7 +215,7 @@
 
 
 def assimilate_kernel(
-    core_ref, own_ref, other_ref, kept_ref, rho_ref, decay_ref, x_ref, x_mean_ref, value_ref, var_ref,
+    own_ref, other_ref, kept_ref, rho_ref, decay_ref, x_ref, x_mean_ref, value_ref, var_ref,
     out_ref, q_ref, s0_ref, s1_ref, t_ref, c_ref, g_ref, mean_ref, panel_ref, swept_ref, trans_ref,
     v_ref, innov_ref, w_ref, v1_ref, e_ref, stage_ref, sems,
 ):
@@ -221,7 +225,7 @@
     per_dev = n // ncols
     groups = per_dev // 8
     chunks = members // 128
-    core = core_ref[0]
+    core = lax.axis_index("row") & 1
     scale = 1.0 / (members - 1.0)
     obs1, obs0 = rows_dev, rows_dev + n
 
@@ -391,25 +395,25 @@
     return jax.ShapeDtypeStruct(shape, jnp.float32)
 
 
-def prepare(first, owner, taper_mask, ensemble, obs_rows, obs_value, obs_var, ncols, local_len):
+def prepare(owner, taper_mask, ensemble, obs_rows, obs_value, obs_var, nrows, ncols, local_len):
     rows_dev, members = ensemble.shape
     n = obs_rows.shape[1]
     return on_core(
-        functools.partial(prepare_kernel, ncols=ncols, local_len=local_len), "prepare",
-        (floats(2, rows_dev, n), floats(n, n), floats(rows_dev, members), floats(rows_dev, 128),
+        functools.partial(prepare_kernel, nrows=nrows, ncols=ncols, local_len=local_len), "prepare",
+        (jax.ShapeDtypeStruct((1, 1024 + 128), jnp.int32), floats(2, rows_dev, n), floats(n, n), floats(rows_dev, members), floats(rows_dev, 128),
          floats(n, 128), floats(2, n)),
-        (first, owner, taper_mask), (ensemble, obs_rows, obs_value, obs_var), limit_mib=None,
-    )
-
-
-def assimilate(core, own, other, kept, prepared):
+        (owner, taper_mask), (ensemble, obs_rows, obs_value, obs_var), limit_mib=None,
+    )
+
+
+def assimilate(own, other, kept, prepared):
     rows_dev, members = prepared[2].shape
     n = prepared[1].shape[0]
     total = rows_dev + 2 * n
     return pl.pallas_call(
         assimilate_kernel,
         out_shape=floats(rows_dev, members),
-        in_specs=[pl.BlockSpec(memory_space=SMEM)] + [pl.BlockSpec(memory_space=VMEM)] * (3 + len(prepared)),
+        in_specs=[pl.BlockSpec(memory_space=VMEM)] * (3 + len(prepared)),
         out_specs=pl.BlockSpec(memory_space=pl.ANY),
         scratch_shapes=[
             VMEM((rows_dev + n, members), jnp.float32),
@@ -432,26 +436,23 @@
         ],
         compiler_params=pltpu.CompilerParams(vmem_limit_bytes=40 * 1024 * 1024),
         name="assimilate",
-    )(core, own, other, kept, *prepared)
+    )(own, other, kept, *prepared)
 
 
 def on_device(ensemble, obs_rows, owner, obs_value, obs_var, taper_mask):
     rows, members = ensemble.shape
     ncols, nrows = lax.axis_size("col"), lax.axis_size("row")
-    my_row, my_col = lax.axis_index("row"), lax.axis_index("col")
     per_dev = obs_rows.shape[1] // ncols
     picked = on_core(
         pick_kernel, "pick_rows", floats(nrows, 1, 1024 + 128),
-        (obs_rows, my_col[None], taper_mask), (ensemble,), [VMEM((2 * per_dev, members), jnp.float32)], None,
+        (obs_rows, taper_mask), (ensemble,), [VMEM((2 * per_dev, members), jnp.float32)], None,
     )
     pieces = exchange(picked, "row")
-    first, core = ((my_row * ncols + my_col) * rows)[None], (my_row & 1)[None]
-    prepared = prepare(first, owner, taper_mask, ensemble, obs_rows, obs_value, obs_var, ncols, rows * nrows * ncols // 4)
-    source = jnp.where(my_row < nrows // 2, owner[0], owner[1])
-    pieces, *prepared = lax.optimization_barrier((pieces, *prepared))
-    tile = lax.dynamic_index_in_dim(pieces, source, 0)[:, :, :1024]
-    mask = lax.dynamic_index_in_dim(pieces, owner[1], 0)[:, :, 1024:]
-    line = jnp.broadcast_to(jnp.concatenate([tile, mask], axis=2), (ncols, 1, 1024 + 128))
+    prepared = prepare(owner, taper_mask, ensemble, obs_rows, obs_value, obs_var, nrows, ncols, rows * nrows * ncols // 4)
+    pieces, wanted, *prepared = lax.optimization_barrier((pieces, *prepared))
+    taken = jnp.arange(nrows, dtype=jnp.int32)[:, None, None] == wanted[None]
+    line = jnp.sum(jnp.where(taken, pieces, 0.0), axis=0)
+    line = jnp.broadcast_to(line[None], (ncols, 1, 1024 + 128))
     line = exchange(line, "col")
     wide, kept = on_core(
         share_kernel, "share", (floats(nrows // 2, ncols, 8, 128), floats(ncols, 128)),
@@ -459,7 +460,7 @@
     )
     own = exchange(wide, "row", [[r for r in range(nrows) if r % 2 == c] for c in range(2)])
     other = lax.ppermute(own, "row", [(r, r ^ 1) for r in range(nrows)])
-    return assimilate(core, own, other, kept, prepared)
+    return assimilate(own, other, kept, prepared)
 
 
 def solution(mesh):

time: 94.5 us -> 91.9 us (0.972)
  waiting for transfers between devices: 3.33 us -> 7.77 us
  between operations: 3.31 us -> 0.11 us
  blocking collectives: 45.8 us -> 43.1 us
    all_to_all x1, waiting for transfers between devices: 1.08 us -> 5.51 us  [exchange(): lax.all_to_all(x, axis, split_axis=0, concat_axis=0, axis_index_groups=gr...]
    all_to_all x2, blocking collectives: 45.8 us -> 43.1 us  [exchange(): lax.all_to_all(x, axis, split_axis=0, concat_axis=0, axis_index_groups=gr...]
  transfers between devices with their start and end apart: 2 -> 2, of which waited for: 2 -> 2; matrix products, arithmetic and copies ran while one was open for 1% -> 0% of each run, Pallas kernels for 2% -> 3%
where the time goes in v6:
time: 91.9 us; the launch traced here: 91.6 us
  blocking collectives  43.1 us (47%)
  Pallas kernels  24.5 us (27%)
  starting transfers between devices  15.2 us (17%)
  waiting for transfers between devices  7.77 us (8%)
    all_to_all x2, blocking collectives, exchange(): lax.all_to_all(x, axis, split_axis=0, concat_axis=0, axis_index_groups=gr...  43.1 us
    pallas_call x1, Pallas kernels, assimilate(): pl.pallas_call(assimilate_kernel, out_shape=floats(rows_dev, members), in...  20.2 us
    all_to_all x1, starting transfers between devices, exchange(): lax.all_to_all(x, axis, split_axis=0, concat_axis=0, axis_index_groups=gr...  10.3 us
    all_to_all x1, waiting for transfers between devices, exchange(): lax.all_to_all(x, axis, split_axis=0, concat_axis=0, axis_index_groups=gr...  5.51 us
    ppermute x1, starting transfers between devices, on_device(): other = lax.ppermute(own, 'row', [(r, r ^ 1) for r in range(nrows)])  4.8 us
    pallas_call x3, Pallas kernels, on_core(): pl.pallas_call(kernel, out_shape=outs, in_specs=[pl.BlockSpec(memory_spac...  4.32 us
    ppermute x1, waiting for transfers between devices, on_device(): other = lax.ppermute(own, 'row', [(r, r ^ 1) for r in range(nrows)])  2.26 us
  transfers between devices with their start and end apart: 2, of which 2 were waited for; matrix products, arithmetic and copies ran while one was open for 0% of the time, Pallas kernels for 3%

profile of v6, /device:TPU:1, one launch (start us, length us, event | category | flops | bytes accessed | tf_op | source)
XLA Modules:
  0.0 91.6 jit_solution(10041826903669191639)
XLA Ops:
  0.0 1.9 %pick_rows.1 = f32[32,1,1152]{2,1,0:T(1,128)} custom-call(s32[2,256]{1,0:T(2,128)} %rows_ref.3, s32[2,1,2]{2,1,0:T(1,128)} %mask_ref.3, f32[128,1024]{1,0:T(8,128)} %x_ref.3), custom_call_target="tpu_custom_call" | custom-call | tf_op jit(solution)/shard_map/pick_rows/pallas_call | solution.py:379
  1.9 10.3 %all-to-all-start = ((f32[32,1,1152]{2,1,0:T(1,128)}), f32[32,1,1152]{2,1,0:T(1,128)S(1)}, u32[]{:S(2)}, u32[]{:S(2)}) async-start(f32[32,1,1152]{2,1,0:T(1,128)} %pick_rows.1), calls=%async_computation | async-start | bytes 294912 | tf_op jit(solution)/shard_map/all_to_all | solution.py:391
  12.2 2.4 %prepare.1 = (s32[1,1152]{1,0:T(1,128)}, f32[2,128,256]{2,1,0:T(8,128)}, f32[256,256]{1,0:T(8,128)}, f32[128,1024]{1,0:T(8,128)}, f32[128,128]{1,0:T(8,128)}, /*index=5*/f32[256,128]{1,0:T(8,128)}, f32[2,256]{1,0:T(2,128)}) custom-call(s32[2]{0:T(128)} %owner_ref.1, s32[2,1,2]{2,1,0:T(1,128)} %mask_ref.3, f32[128,1024]{1,0:T(8,128)} %x_ref.3, ...), custom_call_target="tpu_custom_call" | custom-call | tf_op jit(solution)/shard_map/prepare/pallas_call | solution.py:379
  14.6 5.5 %all-to-all-done = f32[32,1,1152]{2,1,0:T(1,128)S(1)} async-done(((f32[32,1,1152]{2,1,0:T(1,128)}), f32[32,1,1152]{2,1,0:T(1,128)S(1)}, u32[]{:S(2)}, u32[]{:S(2)}) %all-to-all-start) | async-done | bytes 147488 | tf_op jit(solution)/shard_map/all_to_all | solution.py:391
  20.1 0.0 copy-start.6
  20.1 0.7 copy-done.6
  20.8 0.2 fusion
  21.0 24.6 %all_to_all.15.line_ref = f32[16,1,1152]{2,1,0:T(1,128)S(1)} all-to-all(f32[16,1,1152]{2,1,0:T(1,128)S(1)} %broadcast_in_dim.7), channel_id=1, replica_groups=mesh['row'=32,'col'=16] {'col'}, dimensions={0} | all-to-all | bytes 147456 | tf_op jit(solution)/shard_map/all_to_all | solution.py:391
  45.6 0.1 share.1
  45.7 0.0 copy-start
  45.7 0.0 copy-start.1
  45.7 0.0 copy-start.2
  45.7 0.0 copy-start.3
  45.7 0.0 copy-start.4
  45.7 0.0 copy-start.5
  45.7 18.5 %all_to_all.16.own_ref = f32[16,16,8,128]{3,2,1,0:T(8,128)S(1)} all-to-all(f32[16,16,8,128]{3,2,1,0:T(8,128)S(1)} %get-tuple-element.31), channel_id=1, replica_groups={{0,32,64,96,128,160,192,224,256,288,320,352,384,416,448,480},{16,48,80,..., dimensions={0} | all-to-all | bytes 2097152 | tf_op jit(solution)/shard_map/all_to_all | solution.py:391
  64.3 4.8 %collective-permute-start = (f32[16,16,8,128]{3,2,1,0:T(8,128)S(1)}, f32[16,16,8,128]{3,2,1,0:T(8,128)S(1)}, u32[]{:S(2)}, u32[]{:S(2)}) collective-permute-start(f32[16,16,8,128]{3,2,1,0:T(8,128)S(1)} %all_to_all.16.own_ref), channel_id=1, source_target_pairs={{0,16},{16,0},{32,48},{48,32},{64,80},{80,64},{96,112},{112,96},{1... | collective-permute-start | bytes 3145736 | tf_op jit(solution)/shard_map/ppermute | solution.py:462
  69.1 2.3 %collective-permute-done.other_ref = f32[16,16,8,128]{3,2,1,0:T(8,128)S(1)} collective-permute-done((f32[16,16,8,128]{3,2,1,0:T(8,128)S(1)}, f32[16,16,8,128]{3,2,1,0:T(8,128)S(1)}, u32[]{:S(2)}, u32[]{:S(2)}) %collective-permute-start) | collective-permute-done | bytes 1048608 | tf_op jit(solution)/shard_map/ppermute | solution.py:462
  71.3 0.0 copy-done
  71.4 0.0 copy-done.1
  71.4 0.0 copy-done.2
  71.4 0.0 copy-done.3
  71.4 0.0 copy-done.4
  71.4 0.0 copy-done.5
  71.4 20.2 %assimilate.1 = f32[128,1024]{1,0:T(8,128)} custom-call(f32[16,16,8,128]{3,2,1,0:T(8,128)S(1)} %all_to_all.16.own_ref, f32[16,16,8,128]{3,2,1,0:T(8,128)S(1)} %collective-permute-done.other_ref, f32[16,128]{1,0:T(8,128)S(1)} %get-tuple-element.32.kept_ref, f32[2,128,256]{2,1,0:T(8,128)S(1)} %copy-done.1, f32[256,256]{1,0:T(8,128)S(1)} %copy-done.2, ...), custom_call_target="tpu_custom_call" | custom-call | tf_op jit(solution)/shard_map/assimilate/pallas_call | solution.py:413
  (2 shorter events, 0.1 us)
Async XLA Ops:
  1.9 18.2 %all-to-all-start = ((f32[32,1,1152]{2,1,0:T(1,128)}), f32[32,1,1152]{2,1,0:T(1,128)S(1)}, u32[]{:S(2)}, u32[]{:S(2)}) async-start(f32[32,1,1152]{2,1,0:T(1,128)} %pick_rows.1), calls=%async_computation | async-start | bytes 294912 | tf_op jit(solution)/shard_map/all_to_all | solution.py:391
  20.1 0.7 copy-start.6
  45.7 25.7 %copy-start = (f32[128,1024]{1,0:T(8,128)S(1)}, f32[128,1024]{1,0:T(8,128)}, u32[]{:S(2)}) copy-start(f32[128,1024]{1,0:T(8,128)} %get-tuple-element.35.x_ref) | copy-start | bytes 1572868
  45.7 25.7 %copy-start.1 = (f32[2,128,256]{2,1,0:T(8,128)S(1)}, f32[2,128,256]{2,1,0:T(8,128)}, u32[]{:S(2)}) copy-start(f32[2,128,256]{2,1,0:T(8,128)} %get-tuple-element.33.rho_ref) | copy-start | bytes 786436
  45.7 25.6 %copy-start.2 = (f32[256,256]{1,0:T(8,128)S(1)}, f32[256,256]{1,0:T(8,128)}, u32[]{:S(2)}) copy-start(f32[256,256]{1,0:T(8,128)} %get-tuple-element.34.decay_ref) | copy-start | bytes 786436
  45.7 25.6 %copy-start.3 = (f32[256,128]{1,0:T(8,128)S(1)}, f32[256,128]{1,0:T(8,128)}, u32[]{:S(2)}) copy-start(f32[256,128]{1,0:T(8,128)} %get-tuple-element.37.value_ref) | copy-start | bytes 393220
  45.7 25.6 %copy-start.4 = (f32[128,128]{1,0:T(8,128)S(1)}, f32[128,128]{1,0:T(8,128)}, u32[]{:S(2)}) copy-start(f32[128,128]{1,0:T(8,128)} %get-tuple-element.36.x_mean_ref) | copy-start | bytes 196612
  45.7 25.6 %copy-start.5 = (f32[2,256]{1,0:T(2,128)S(1)}, f32[2,256]{1,0:T(2,128)}, u32[]{:S(2)}) copy-start(f32[2,256]{1,0:T(2,128)} %get-tuple-element.38.var_ref) | copy-start | bytes 6148
  64.3 7.1 %collective-permute-start = (f32[16,16,8,128]{3,2,1,0:T(8,128)S(1)}, f32[16,16,8,128]{3,2,1,0:T(8,128)S(1)}, u32[]{:S(2)}, u32[]{:S(2)}) collective-permute-start(f32[16,16,8,128]{3,2,1,0:T(8,128)S(1)} %all_to_all.16.own_ref), channel_id=1, source_target_pairs={{0,16},{16,0},{32,48},{48,32},{64,80},{80,64},{96,112},{112,96},{1... | collective-permute-start | bytes 3145736 | tf_op jit(solution)/shard_map/ppermute | solution.py:462

commit v7 on v6

--- a/solution.py
+++ b/solution.py
@@ -165,6 +165,12 @@
         out_ref[piece, :, 1024:] = kept
 
 
+def choose_kernel(owner_ref, wanted_ref, *, nrows):
+    place = lax.broadcasted_iota(jnp.int32, wanted_ref.shape, 1)
+    early = lax.axis_index("row") < nrows // 2
+    wanted_ref[...] = jnp.where((place < 1024) & early, owner_ref[0], owner_ref[1])
+
+
 def share_kernel(line_ref, out_ref, kept_ref, held):
     for c in range(line_ref.shape[0]):
         for s in range(8):
@@ -176,14 +182,11 @@
 
 def prepare_kernel(
     owner_ref, mask_ref, x_ref, rows_ref, given_ref, var_ref,
-    wanted_ref, rho_ref, decay_ref, anom_ref, mean_ref, value_ref, held_var_ref, *, nrows, ncols, local_len,
+    rho_ref, decay_ref, anom_ref, mean_ref, value_ref, held_var_ref, *, ncols, local_len,
 ):
     rows_dev, members = x_ref.shape
     n = rows_ref.shape[1]
     per_dev = n // ncols
-    place = lax.broadcasted_iota(jnp.int32, wanted_ref.shape, 1)
-    early = lax.axis_index("row") < nrows // 2
-    wanted_ref[...] = jnp.where((place < 1024) & early, owner_ref[0], owner_ref[1])
     lane = lax.broadcasted_iota(jnp.int32, (1, n), 1)
     first = (lax.axis_index("row") * ncols + lax.axis_index("col")) * rows_dev
     here = first + lax.broadcasted_iota(jnp.int32, (rows_dev, 1), 0)
@@ -250,7 +253,7 @@
                 mean_ref[pl.ds(pl.multiple_of(top + c * per_dev + g * 8, 8), 8), :] = total
         return carry
 
-    lax.fori_loop(0, ncols, add_up, 0)
+    lax.fori_loop(0, ncols, add_up, 0, unroll=4)
     mean = jnp.sum(mean_ref[obs1:, :], axis=1, keepdims=True) * (1.0 / members)
     mean_ref[obs1:, :] = jnp.broadcast_to(mean, (2 * n, 128))
     mean_ref[:rows_dev, :] = x_mean_ref[...]
@@ -268,7 +271,7 @@
         c_ref[...] += dot_parts(parts, parts, 1)
         return carry
 
-    lax.fori_loop(0, members // wide, covariance0, 0)
+    lax.fori_loop(0, members // wide, covariance0, 0, unroll=4)
     for p, part in enumerate(split(c_ref[...], 3)):
         w_ref[p] = part
     c_ref[...] = c_ref[...] * scale + jnp.where(diag, var_ref[0:1, :], 0.0)
@@ -395,12 +398,12 @@
     return jax.ShapeDtypeStruct(shape, jnp.float32)
 
 
-def prepare(owner, taper_mask, ensemble, obs_rows, obs_value, obs_var, nrows, ncols, local_len):
+def prepare(owner, taper_mask, ensemble, obs_rows, obs_value, obs_var, ncols, local_len):
     rows_dev, members = ensemble.shape
     n = obs_rows.shape[1]
     return on_core(
-        functools.partial(prepare_kernel, nrows=nrows, ncols=ncols, local_len=local_len), "prepare",
-        (jax.ShapeDtypeStruct((1, 1024 + 128), jnp.int32), floats(2, rows_dev, n), floats(n, n), floats(rows_dev, members), floats(rows_dev, 128),
+        functools.partial(prepare_kernel, ncols=ncols, local_len=local_len), "prepare",
+        (floats(2, rows_dev, n), floats(n, n), floats(rows_dev, members), floats(rows_dev, 128),
          floats(n, 128), floats(2, n)),
         (owner, taper_mask), (ensemble, obs_rows, obs_value, obs_var), limit_mib=None,
     )
@@ -448,8 +451,12 @@
         (obs_rows, taper_mask), (ensemble,), [VMEM((2 * per_dev, members), jnp.float32)], None,
     )
     pieces = exchange(picked, "row")
-    prepared = prepare(owner, taper_mask, ensemble, obs_rows, obs_value, obs_var, nrows, ncols, rows * nrows * ncols // 4)
-    pieces, wanted, *prepared = lax.optimization_barrier((pieces, *prepared))
+    prepared = prepare(owner, taper_mask, ensemble, obs_rows, obs_value, obs_var, ncols, rows * nrows * ncols // 4)
+    wanted = on_core(
+        functools.partial(choose_kernel, nrows=nrows), "choose",
+        jax.ShapeDtypeStruct((1, 1024 + 128), jnp.int32), (owner,), (),
+    )
+    pieces, wanted, *prepared = lax.optimization_barrier((pieces, wanted, *prepared))
     taken = jnp.arange(nrows, dtype=jnp.int32)[:, None, None] == wanted[None]
     line = jnp.sum(jnp.where(taken, pieces, 0.0), axis=0)
     line = jnp.broadcast_to(line[None], (ncols, 1, 1024 + 128))

time: 91.9 us -> 90.5 us (0.985)
    pallas_call x3 -> x4, Pallas kernels: 4.32 us -> 4.85 us  [on_core(): pl.pallas_call(kernel, out_shape=outs, in_specs=[pl.BlockSpec(memory_spac...]
where the time goes in v7:
time: 90.5 us; the launch traced here: 90.2 us
  blocking collectives  43.1 us (48%)
  Pallas kernels  24.2 us (27%)
  starting transfers between devices  15.3 us (17%)
  waiting for transfers between devices  7.22 us (8%)
    all_to_all x2, blocking collectives, exchange(): lax.all_to_all(x, axis, split_axis=0, concat_axis=0, axis_index_groups=gr...  43.1 us
    pallas_call x1, Pallas kernels, assimilate(): pl.pallas_call(assimilate_kernel, out_shape=floats(rows_dev, members), in...  19.4 us
    all_to_all x1, starting transfers between devices, exchange(): lax.all_to_all(x, axis, split_axis=0, concat_axis=0, axis_index_groups=gr...  10.5 us
    all_to_all x1, waiting for transfers between devices, exchange(): lax.all_to_all(x, axis, split_axis=0, concat_axis=0, axis_index_groups=gr...  4.96 us
    pallas_call x4, Pallas kernels, on_core(): pl.pallas_call(kernel, out_shape=outs, in_specs=[pl.BlockSpec(memory_spac...  4.85 us
    ppermute x1, starting transfers between devices, on_device(): other = lax.ppermute(own, 'row', [(r, r ^ 1) for r in range(nrows)])  4.8 us
    ppermute x1, waiting for transfers between devices, on_device(): other = lax.ppermute(own, 'row', [(r, r ^ 1) for r in range(nrows)])  2.26 us
  transfers between devices with their start and end apart: 2, of which 2 were waited for; matrix products, arithmetic and copies ran while one was open for 0% of the time, Pallas kernels for 3%

profile of v7, /device:TPU:1, one launch (start us, length us, event | category | flops | bytes accessed | tf_op | source)
XLA Modules:
  0.0 90.2 jit_solution(7609349007500509319)
XLA Ops:
  0.0 1.9 %pick_rows.1 = f32[32,1,1152]{2,1,0:T(1,128)} custom-call(s32[2,256]{1,0:T(2,128)} %rows_ref.3, s32[2,1,2]{2,1,0:T(1,128)} %mask_ref.3, f32[128,1024]{1,0:T(8,128)} %x_ref.3), custom_call_target="tpu_custom_call" | custom-call | tf_op jit(solution)/shard_map/pick_rows/pallas_call | solution.py:382
  1.9 0.0 copy-start.6
  1.9 10.5 %all-to-all-start = ((f32[32,1,1152]{2,1,0:T(1,128)}), f32[32,1,1152]{2,1,0:T(1,128)S(1)}, u32[]{:S(2)}, u32[]{:S(2)}) async-start(f32[32,1,1152]{2,1,0:T(1,128)} %pick_rows.1), calls=%async_computation | async-start | bytes 294912 | tf_op jit(solution)/shard_map/all_to_all | solution.py:394
  12.4 0.0 copy-done.6
  12.4 0.6 choose.1
  12.9 2.3 %prepare.1 = (f32[2,128,256]{2,1,0:T(8,128)}, f32[256,256]{1,0:T(8,128)}, f32[128,1024]{1,0:T(8,128)}, f32[128,128]{1,0:T(8,128)}, f32[256,128]{1,0:T(8,128)}, /*index=5*/f32[2,256]{1,0:T(2,128)}) custom-call(s32[2]{0:T(128)} %owner_ref.3, s32[2,1,2]{2,1,0:T(1,128)} %mask_ref.3, f32[128,1024]{1,0:T(8,128)} %x_ref.3, s32[2,256]{1,0:T(2,128)} %rows_ref.3, ...), custom_call_target="tpu_custom_call" | custom-call | tf_op jit(solution)/shard_map/prepare/pallas_call | solution.py:382
  15.3 5.0 %all-to-all-done = f32[32,1,1152]{2,1,0:T(1,128)S(1)} async-done(((f32[32,1,1152]{2,1,0:T(1,128)}), f32[32,1,1152]{2,1,0:T(1,128)S(1)}, u32[]{:S(2)}, u32[]{:S(2)}) %all-to-all-start) | async-done | bytes 147488 | tf_op jit(solution)/shard_map/all_to_all | solution.py:394
  20.3 0.2 fusion
  20.5 24.6 %all_to_all.15.line_ref = f32[16,1,1152]{2,1,0:T(1,128)S(1)} all-to-all(f32[16,1,1152]{2,1,0:T(1,128)S(1)} %broadcast_in_dim.7), channel_id=1, replica_groups=mesh['row'=32,'col'=16] {'col'}, dimensions={0} | all-to-all | bytes 147456 | tf_op jit(solution)/shard_map/all_to_all | solution.py:394
  45.0 0.1 share.1
  45.1 0.0 copy-start
  45.1 0.0 copy-start.1
  45.2 0.0 copy-start.2
  45.2 0.0 copy-start.3
  45.2 0.0 copy-start.4
  45.2 0.0 copy-start.5
  45.2 18.5 %all_to_all.16.own_ref = f32[16,16,8,128]{3,2,1,0:T(8,128)S(1)} all-to-all(f32[16,16,8,128]{3,2,1,0:T(8,128)S(1)} %get-tuple-element.29), channel_id=1, replica_groups={{0,32,64,96,128,160,192,224,256,288,320,352,384,416,448,480},{16,48,80,..., dimensions={0} | all-to-all | bytes 2097152 | tf_op jit(solution)/shard_map/all_to_all | solution.py:394
  63.7 4.8 %collective-permute-start = (f32[16,16,8,128]{3,2,1,0:T(8,128)S(1)}, f32[16,16,8,128]{3,2,1,0:T(8,128)S(1)}, u32[]{:S(2)}, u32[]{:S(2)}) collective-permute-start(f32[16,16,8,128]{3,2,1,0:T(8,128)S(1)} %all_to_all.16.own_ref), channel_id=1, source_target_pairs={{0,16},{16,0},{32,48},{48,32},{64,80},{80,64},{96,112},{112,96},{1... | collective-permute-start | bytes 3145736 | tf_op jit(solution)/shard_map/ppermute | solution.py:469
  68.5 2.3 %collective-permute-done.other_ref = f32[16,16,8,128]{3,2,1,0:T(8,128)S(1)} collective-permute-done((f32[16,16,8,128]{3,2,1,0:T(8,128)S(1)}, f32[16,16,8,128]{3,2,1,0:T(8,128)S(1)}, u32[]{:S(2)}, u32[]{:S(2)}) %collective-permute-start) | collective-permute-done | bytes 1048608 | tf_op jit(solution)/shard_map/ppermute | solution.py:469
  70.8 0.0 copy-done
  70.8 0.0 copy-done.1
  70.8 0.0 copy-done.2
  70.8 0.0 copy-done.3
  70.8 0.0 copy-done.4
  70.8 0.0 copy-done.5
  70.8 19.4 %assimilate.1 = f32[128,1024]{1,0:T(8,128)} custom-call(f32[16,16,8,128]{3,2,1,0:T(8,128)S(1)} %all_to_all.16.own_ref, f32[16,16,8,128]{3,2,1,0:T(8,128)S(1)} %collective-permute-done.other_ref, f32[16,128]{1,0:T(8,128)S(1)} %get-tuple-element.30.kept_ref, f32[2,128,256]{2,1,0:T(8,128)S(1)} %copy-done.1, f32[256,256]{1,0:T(8,128)S(1)} %copy-done.2, ...), custom_call_target="tpu_custom_call" | custom-call | tf_op jit(solution)/shard_map/assimilate/pallas_call | solution.py:416
  (2 shorter events, 0.1 us)
Async XLA Ops:
  1.9 10.5 %copy-start.6 = (s32[2]{0:T(128)S(1)}, s32[2]{0:T(128)}, u32[]{:S(2)}) copy-start(s32[2]{0:T(128)} %owner_ref.3) | copy-start | bytes 28
  1.9 18.4 %all-to-all-start = ((f32[32,1,1152]{2,1,0:T(1,128)}), f32[32,1,1152]{2,1,0:T(1,128)S(1)}, u32[]{:S(2)}, u32[]{:S(2)}) async-start(f32[32,1,1152]{2,1,0:T(1,128)} %pick_rows.1), calls=%async_computation | async-start | bytes 294912 | tf_op jit(solution)/shard_map/all_to_all | solution.py:394
  45.1 25.7 %copy-start = (f32[128,1024]{1,0:T(8,128)S(1)}, f32[128,1024]{1,0:T(8,128)}, u32[]{:S(2)}) copy-start(f32[128,1024]{1,0:T(8,128)} %get-tuple-element.33.x_ref) | copy-start | bytes 1572868
  45.1 25.7 %copy-start.1 = (f32[2,128,256]{2,1,0:T(8,128)S(1)}, f32[2,128,256]{2,1,0:T(8,128)}, u32[]{:S(2)}) copy-start(f32[2,128,256]{2,1,0:T(8,128)} %get-tuple-element.31.rho_ref) | copy-start | bytes 786436
  45.2 25.6 %copy-start.2 = (f32[256,256]{1,0:T(8,128)S(1)}, f32[256,256]{1,0:T(8,128)}, u32[]{:S(2)}) copy-start(f32[256,256]{1,0:T(8,128)} %get-tuple-element.32.decay_ref) | copy-start | bytes 786436
  45.2 25.6 %copy-start.3 = (f32[256,128]{1,0:T(8,128)S(1)}, f32[256,128]{1,0:T(8,128)}, u32[]{:S(2)}) copy-start(f32[256,128]{1,0:T(8,128)} %get-tuple-element.35.value_ref) | copy-start | bytes 393220
  45.2 25.6 %copy-start.4 = (f32[128,128]{1,0:T(8,128)S(1)}, f32[128,128]{1,0:T(8,128)}, u32[]{:S(2)}) copy-start(f32[128,128]{1,0:T(8,128)} %get-tuple-element.34.x_mean_ref) | copy-start | bytes 196612
  45.2 25.6 %copy-start.5 = (f32[2,256]{1,0:T(2,128)S(1)}, f32[2,256]{1,0:T(2,128)}, u32[]{:S(2)}) copy-start(f32[2,256]{1,0:T(2,128)} %get-tuple-element.36.var_ref) | copy-start | bytes 6148
  63.7 7.1 %collective-permute-start = (f32[16,16,8,128]{3,2,1,0:T(8,128)S(1)}, f32[16,16,8,128]{3,2,1,0:T(8,128)S(1)}, u32[]{:S(2)}, u32[]{:S(2)}) collective-permute-start(f32[16,16,8,128]{3,2,1,0:T(8,128)S(1)} %all_to_all.16.own_ref), channel_id=1, source_target_pairs={{0,16},{16,0},{32,48},{48,32},{64,80},{80,64},{96,112},{112,96},{1... | collective-permute-start | bytes 3145736 | tf_op jit(solution)/shard_map/ppermute | solution.py:469

commit v8 on v7

--- a/solution.py
+++ b/solution.py
@@ -282,13 +282,12 @@
         at, i, side = chunk(j, 128), j // 2, j % 2
         local = jnp.where(side == 0, x_ref[:, member_chunk(i, 0)], x_ref[:, member_chunk(i, 1)])
         seen = jnp.where(side == 0, observed(1, i, own_ref), observed(1, i, other_ref))
-        for top, anom in ((0, local), (obs1, seen - mean_ref[obs1:obs0, :])):
-            rows = slice(top, top + anom.shape[0])
-            q_ref[rows, at] = anom
-            parts = split(anom, 3)
-            t_ref[rows, :] += dot_parts(parts, [s0_ref[p, :, at] for p in range(3)], 1)
-            if top:
-                e_ref[...] += dot_parts(parts, parts, 1)
+        anom = jnp.concatenate([local, seen - mean_ref[obs1:obs0, :]], axis=0)
+        q_ref[:, at] = anom
+        parts = split(anom, 3)
+        t_ref[...] += dot_parts(parts, [s0_ref[p, :, at] for p in range(3)], 1)
+        parts = [part[obs1:] for part in parts]
+        e_ref[...] += dot_parts(parts, parts, 1)
 
     invert_in_place(c_ref, panel_ref, swept_ref, trans_ref, cross0)
 

time: 90.5 us -> 90.3 us (level)
  no operation moved by 1% of the time
where the time goes in v8:
time: 90.3 us; the launch traced here: 90 us
  blocking collectives  43.1 us (48%)
  Pallas kernels  24 us (27%)
  starting transfers between devices  15.3 us (17%)
  waiting for transfers between devices  7.22 us (8%)
    all_to_all x2, blocking collectives, exchange(): lax.all_to_all(x, axis, split_axis=0, concat_axis=0, axis_index_groups=gr...  43.1 us
    pallas_call x1, Pallas kernels, assimilate(): pl.pallas_call(assimilate_kernel, out_shape=floats(rows_dev, members), in...  19.1 us
    all_to_all x1, starting transfers between devices, exchange(): lax.all_to_all(x, axis, split_axis=0, concat_axis=0, axis_index_groups=gr...  10.5 us
    all_to_all x1, waiting for transfers between devices, exchange(): lax.all_to_all(x, axis, split_axis=0, concat_axis=0, axis_index_groups=gr...  4.96 us
    pallas_call x4, Pallas kernels, on_core(): pl.pallas_call(kernel, out_shape=outs, in_specs=[pl.BlockSpec(memory_spac...  4.85 us
    ppermute x1, starting transfers between devices, on_device(): other = lax.ppermute(own, 'row', [(r, r ^ 1) for r in range(nrows)])  4.8 us
    ppermute x1, waiting for transfers between devices, on_device(): other = lax.ppermute(own, 'row', [(r, r ^ 1) for r in range(nrows)])  2.26 us
  transfers between devices with their start and end apart: 2, of which 2 were waited for; matrix products, arithmetic and copies ran while one was open for 0% of the time, Pallas kernels for 3%

profile of v8, /device:TPU:1, one launch (start us, length us, event | category | flops | bytes accessed | tf_op | source)
XLA Modules:
  0.0 90.0 jit_solution(6472921379701755842)
XLA Ops:
  0.0 1.9 %pick_rows.1 = f32[32,1,1152]{2,1,0:T(1,128)} custom-call(s32[2,256]{1,0:T(2,128)} %rows_ref.3, s32[2,1,2]{2,1,0:T(1,128)} %mask_ref.3, f32[128,1024]{1,0:T(8,128)} %x_ref.3), custom_call_target="tpu_custom_call" | custom-call | tf_op jit(solution)/shard_map/pick_rows/pallas_call | solution.py:381
  1.9 0.0 copy-start.6
  1.9 10.5 %all-to-all-start = ((f32[32,1,1152]{2,1,0:T(1,128)}), f32[32,1,1152]{2,1,0:T(1,128)S(1)}, u32[]{:S(2)}, u32[]{:S(2)}) async-start(f32[32,1,1152]{2,1,0:T(1,128)} %pick_rows.1), calls=%async_computation | async-start | bytes 294912 | tf_op jit(solution)/shard_map/all_to_all | solution.py:393
  12.4 0.0 copy-done.6
  12.4 0.6 choose.1
  12.9 2.3 %prepare.1 = (f32[2,128,256]{2,1,0:T(8,128)}, f32[256,256]{1,0:T(8,128)}, f32[128,1024]{1,0:T(8,128)}, f32[128,128]{1,0:T(8,128)}, f32[256,128]{1,0:T(8,128)}, /*index=5*/f32[2,256]{1,0:T(2,128)}) custom-call(s32[2]{0:T(128)} %owner_ref.3, s32[2,1,2]{2,1,0:T(1,128)} %mask_ref.3, f32[128,1024]{1,0:T(8,128)} %x_ref.3, s32[2,256]{1,0:T(2,128)} %rows_ref.3, ...), custom_call_target="tpu_custom_call" | custom-call | tf_op jit(solution)/shard_map/prepare/pallas_call | solution.py:381
  15.3 5.0 %all-to-all-done = f32[32,1,1152]{2,1,0:T(1,128)S(1)} async-done(((f32[32,1,1152]{2,1,0:T(1,128)}), f32[32,1,1152]{2,1,0:T(1,128)S(1)}, u32[]{:S(2)}, u32[]{:S(2)}) %all-to-all-start) | async-done | bytes 147488 | tf_op jit(solution)/shard_map/all_to_all | solution.py:393
  20.3 0.2 fusion
  20.5 24.6 %all_to_all.15.line_ref = f32[16,1,1152]{2,1,0:T(1,128)S(1)} all-to-all(f32[16,1,1152]{2,1,0:T(1,128)S(1)} %broadcast_in_dim.7), channel_id=1, replica_groups=mesh['row'=32,'col'=16] {'col'}, dimensions={0} | all-to-all | bytes 147456 | tf_op jit(solution)/shard_map/all_to_all | solution.py:393
  45.0 0.1 share.1
  45.1 0.0 copy-start
  45.1 0.0 copy-start.1
  45.2 0.0 copy-start.2
  45.2 0.0 copy-start.3
  45.2 0.0 copy-start.4
  45.2 0.0 copy-start.5
  45.2 18.5 %all_to_all.16.own_ref = f32[16,16,8,128]{3,2,1,0:T(8,128)S(1)} all-to-all(f32[16,16,8,128]{3,2,1,0:T(8,128)S(1)} %get-tuple-element.29), channel_id=1, replica_groups={{0,32,64,96,128,160,192,224,256,288,320,352,384,416,448,480},{16,48,80,..., dimensions={0} | all-to-all | bytes 2097152 | tf_op jit(solution)/shard_map/all_to_all | solution.py:393
  63.7 4.8 %collective-permute-start = (f32[16,16,8,128]{3,2,1,0:T(8,128)S(1)}, f32[16,16,8,128]{3,2,1,0:T(8,128)S(1)}, u32[]{:S(2)}, u32[]{:S(2)}) collective-permute-start(f32[16,16,8,128]{3,2,1,0:T(8,128)S(1)} %all_to_all.16.own_ref), channel_id=1, source_target_pairs={{0,16},{16,0},{32,48},{48,32},{64,80},{80,64},{96,112},{112,96},{1... | collective-permute-start | bytes 3145736 | tf_op jit(solution)/shard_map/ppermute | solution.py:468
  68.5 2.3 %collective-permute-done.other_ref = f32[16,16,8,128]{3,2,1,0:T(8,128)S(1)} collective-permute-done((f32[16,16,8,128]{3,2,1,0:T(8,128)S(1)}, f32[16,16,8,128]{3,2,1,0:T(8,128)S(1)}, u32[]{:S(2)}, u32[]{:S(2)}) %collective-permute-start) | collective-permute-done | bytes 1048608 | tf_op jit(solution)/shard_map/ppermute | solution.py:468
  70.8 0.0 copy-done
  70.8 0.0 copy-done.1
  70.8 0.0 copy-done.2
  70.8 0.0 copy-done.3
  70.8 0.0 copy-done.4
  70.8 0.0 copy-done.5
  70.8 19.1 %assimilate.1 = f32[128,1024]{1,0:T(8,128)} custom-call(f32[16,16,8,128]{3,2,1,0:T(8,128)S(1)} %all_to_all.16.own_ref, f32[16,16,8,128]{3,2,1,0:T(8,128)S(1)} %collective-permute-done.other_ref, f32[16,128]{1,0:T(8,128)S(1)} %get-tuple-element.30.kept_ref, f32[2,128,256]{2,1,0:T(8,128)S(1)} %copy-done.1, f32[256,256]{1,0:T(8,128)S(1)} %copy-done.2, ...), custom_call_target="tpu_custom_call" | custom-call | tf_op jit(solution)/shard_map/assimilate/pallas_call | solution.py:415
  (2 shorter events, 0.1 us)
Async XLA Ops:
  1.9 10.5 %copy-start.6 = (s32[2]{0:T(128)S(1)}, s32[2]{0:T(128)}, u32[]{:S(2)}) copy-start(s32[2]{0:T(128)} %owner_ref.3) | copy-start | bytes 28
  1.9 18.4 %all-to-all-start = ((f32[32,1,1152]{2,1,0:T(1,128)}), f32[32,1,1152]{2,1,0:T(1,128)S(1)}, u32[]{:S(2)}, u32[]{:S(2)}) async-start(f32[32,1,1152]{2,1,0:T(1,128)} %pick_rows.1), calls=%async_computation | async-start | bytes 294912 | tf_op jit(solution)/shard_map/all_to_all | solution.py:393
  45.1 25.7 %copy-start = (f32[128,1024]{1,0:T(8,128)S(1)}, f32[128,1024]{1,0:T(8,128)}, u32[]{:S(2)}) copy-start(f32[128,1024]{1,0:T(8,128)} %get-tuple-element.33.x_ref) | copy-start | bytes 1572868
  45.1 25.7 %copy-start.1 = (f32[2,128,256]{2,1,0:T(8,128)S(1)}, f32[2,128,256]{2,1,0:T(8,128)}, u32[]{:S(2)}) copy-start(f32[2,128,256]{2,1,0:T(8,128)} %get-tuple-element.31.rho_ref) | copy-start | bytes 786436
  45.2 25.6 %copy-start.2 = (f32[256,256]{1,0:T(8,128)S(1)}, f32[256,256]{1,0:T(8,128)}, u32[]{:S(2)}) copy-start(f32[256,256]{1,0:T(8,128)} %get-tuple-element.32.decay_ref) | copy-start | bytes 786436
  45.2 25.6 %copy-start.3 = (f32[256,128]{1,0:T(8,128)S(1)}, f32[256,128]{1,0:T(8,128)}, u32[]{:S(2)}) copy-start(f32[256,128]{1,0:T(8,128)} %get-tuple-element.35.value_ref) | copy-start | bytes 393220
  45.2 25.6 %copy-start.4 = (f32[128,128]{1,0:T(8,128)S(1)}, f32[128,128]{1,0:T(8,128)}, u32[]{:S(2)}) copy-start(f32[128,128]{1,0:T(8,128)} %get-tuple-element.34.x_mean_ref) | copy-start | bytes 196612
  45.2 25.6 %copy-start.5 = (f32[2,256]{1,0:T(2,128)S(1)}, f32[2,256]{1,0:T(2,128)}, u32[]{:S(2)}) copy-start(f32[2,256]{1,0:T(2,128)} %get-tuple-element.36.var_ref) | copy-start | bytes 6148
  63.7 7.1 %collective-permute-start = (f32[16,16,8,128]{3,2,1,0:T(8,128)S(1)}, f32[16,16,8,128]{3,2,1,0:T(8,128)S(1)}, u32[]{:S(2)}, u32[]{:S(2)}) collective-permute-start(f32[16,16,8,128]{3,2,1,0:T(8,128)S(1)} %all_to_all.16.own_ref), channel_id=1, source_target_pairs={{0,16},{16,0},{32,48},{48,32},{64,80},{80,64},{96,112},{112,96},{1... | collective-permute-start | bytes 3145736 | tf_op jit(solution)/shard_map/ppermute | solution.py:468
